TPU v7x, 32 devices: a 4x4x1 block of a 4x4x8 slice. The times are simulated.
32 devices in a mesh: dp: 1 (over z), fsdp: 32 (over y, x, core).
Axes of the slice: x: 4, y: 4, z: 1, core: 2. Of those that a mesh axis runs over, the one named last changes fastest.
The devices are a block of a 4x4x8 slice.
Arguments:
- tokens: int32 [32, 64], P(('dp', 'fsdp'))
- embed_table: bfloat16 [32064, 3072], P('fsdp')
- norm_attn: bfloat16 [3072], P('fsdp')
- w_qkv: bfloat16 [3072, 9216], P('fsdp')
- w_out: bfloat16 [3072, 3072], P('fsdp')
- norm_mlp: bfloat16 [3072], P('fsdp')
- w_gate_up: bfloat16 [3072, 16384], P('fsdp')
- w_down: bfloat16 [8192, 3072], P('fsdp')
- rope_scale: float32 [48], replicated
Outputs:
- output 1: bfloat16 [32, 64, 3072], P(('dp', 'fsdp'))
- output 2: bfloat16 [32, 64, 32, 96], P(('dp', 'fsdp'))
- output 3: bfloat16 [32, 64, 32, 96], P(('dp', 'fsdp'))
All inputs are finite; a program needn't handle non-finite values.
Results may differ from a plain program's by a relative error of at most 0.0101458.
Values are sent between devices in bfloat16 or wider.
A program may use at most 768 MiB of HBM per device.

v0:
```python
import jax
import jax.numpy as jnp
from jax import lax
from jax.sharding import PartitionSpec as P

NORM_EPS = 1e-5
ROPE_THETA = 10000.0


def rms_norm(hidden, gain):
    h_f32 = hidden.astype(jnp.float32)
    inv_rms = lax.rsqrt(jnp.mean(h_f32 * h_f32, axis=-1, keepdims=True) + NORM_EPS)
    return (h_f32 * inv_rms * gain.astype(jnp.float32)).astype(jnp.bfloat16)


def apply_rope(proj, rope_scale):
    seq_len = proj.shape[1]
    head_dim = proj.shape[-1]
    half_dim = head_dim // 2
    freq_expo = jnp.arange(half_dim, dtype=jnp.float32) * (2.0 / head_dim)
    inv_freq = 1.0 / (rope_scale * jnp.power(ROPE_THETA, freq_expo))
    angles = jnp.arange(seq_len, dtype=jnp.float32)[:, None] * inv_freq[None, :]
    cos_tab = jnp.cos(angles)[:, None, :]
    sin_tab = jnp.sin(angles)[:, None, :]
    low_half = proj[..., :half_dim]
    high_half = proj[..., half_dim:]
    return jnp.concatenate([low_half * cos_tab - high_half * sin_tab, high_half * cos_tab + low_half * sin_tab], axis=-1)


def decoder_layer(hidden, norm_attn, w_qkv, w_out, norm_mlp, w_gate_up, w_down, rope_scale):
    n_seq = hidden.shape[0]
    seq_len = hidden.shape[1]
    head_dim = 2 * rope_scale.shape[0]
    q_width = w_out.shape[0]
    kv_width = (w_qkv.shape[1] - q_width) // 2
    n_heads = q_width // head_dim
    kv_heads = kv_width // head_dim
    ff_width = w_down.shape[0]
    normed = rms_norm(hidden, norm_attn)
    qkv_proj = jnp.einsum('bld,de->ble', normed, w_qkv, preferred_element_type=jnp.float32)
    query_rot = apply_rope(qkv_proj[..., :q_width].reshape(n_seq, seq_len, n_heads, head_dim), rope_scale).astype(jnp.bfloat16)
    key_rot = apply_rope(qkv_proj[..., q_width:q_width + kv_width].reshape(n_seq, seq_len, kv_heads, head_dim), rope_scale).astype(jnp.bfloat16)
    values = qkv_proj[..., q_width + kv_width:].reshape(n_seq, seq_len, kv_heads, head_dim).astype(jnp.bfloat16)
    q_grouped = query_rot.reshape(n_seq, seq_len, kv_heads, n_heads // kv_heads, head_dim)
    scores = jnp.einsum('bqkgd,bskd->bkgqs', q_grouped, key_rot, preferred_element_type=jnp.float32) * (head_dim ** -0.5)
    causal = jnp.arange(seq_len)[:, None] >= jnp.arange(seq_len)[None, :]
    scores = jnp.where(causal, scores, -jnp.inf)
    scores = scores - jnp.max(scores, axis=-1, keepdims=True)
    weights = jnp.exp(scores)
    attn_probs = (weights / jnp.sum(weights, axis=-1, keepdims=True)).astype(jnp.bfloat16)
    context = jnp.einsum('bkgqs,bskd->bqkgd', attn_probs, values, preferred_element_type=jnp.float32)
    context = context.astype(jnp.bfloat16).reshape(n_seq, seq_len, q_width)
    attn_proj = jnp.einsum('ble,ed->bld', context, w_out, preferred_element_type=jnp.float32)
    resid_mid = (hidden.astype(jnp.float32) + attn_proj).astype(jnp.bfloat16)
    normed_mlp = rms_norm(resid_mid, norm_mlp)
    gate_up = jnp.einsum('bld,df->blf', normed_mlp, w_gate_up, preferred_element_type=jnp.float32)
    mlp_act = (jax.nn.silu(gate_up[..., :ff_width]) * gate_up[..., ff_width:]).astype(jnp.bfloat16)
    down_proj = jnp.einsum('blf,fd->bld', mlp_act, w_down, preferred_element_type=jnp.float32)
    layer_out = (resid_mid.astype(jnp.float32) + down_proj).astype(jnp.bfloat16)
    return layer_out, key_rot, values


def gather_rows(weight):
    return lax.all_gather(weight, 'fsdp', axis=0, tiled=True)


def solution(mesh):
    batch_axes = ('dp', 'fsdp')
    row_spec = P('fsdp', None)

    def device_step(tokens, embed_table, norm_attn, w_qkv, w_out, norm_mlp, w_gate_up, w_down, rope_scale):
        group_tokens = lax.all_gather(tokens, 'fsdp', axis=0, tiled=True)
        shard_rows = embed_table.shape[0]
        local_ids = group_tokens - lax.axis_index('fsdp') * shard_rows
        owned_mask = (local_ids >= 0) & (local_ids < shard_rows)
        table_rows = jnp.take(embed_table, jnp.clip(local_ids, 0, shard_rows - 1), axis=0)
        table_rows = jnp.where(owned_mask[..., None], table_rows, jnp.zeros((), table_rows.dtype))
        hidden = lax.psum_scatter(table_rows, 'fsdp', scatter_dimension=0, tiled=True)
        full_norm_attn = gather_rows(norm_attn)
        full_qkv = gather_rows(w_qkv)
        full_out = gather_rows(w_out)
        full_norm_mlp = gather_rows(norm_mlp)
        full_gate_up = gather_rows(w_gate_up)
        full_down = gather_rows(w_down)
        return decoder_layer(hidden, full_norm_attn, full_qkv, full_out, full_norm_mlp, full_gate_up, full_down, rope_scale)

    return jax.shard_map(
        device_step,
        mesh=mesh,
        in_specs=(P(batch_axes, None), row_spec, P('fsdp'), row_spec, row_spec, P('fsdp'), row_spec, row_spec, P(None)),
        out_specs=(P(batch_axes, None, None), P(batch_axes, None, None, None), P(batch_axes, None, None, None)),
        check_vma=False,
    )
```

profile of v0, /device:TPU:96, one launch (start us, length us, event | category | flops | bytes accessed | tf_op | source)
XLA Modules:
  0.0 884.4 jit_solution(18097785377484092785)
XLA Ops:
  7.2 36.2 %all-gather = s32[32,1,64]{2,1,0:T(1,128)S(1)} all-gather(s32[1,1,64]{2,1,0:T(1,128)} %bitcast.68), channel_id=1, replica_groups=mesh['dp'=1,'fsdp'=32] {'fsdp'}, dimensions={0}, use_global_device_ids=true | all-gather | bytes 8448 | tf_op jit(solution)/shard_map/all_gather | solution.py:72
  43.6 26.5 %gather_fusion = bf16[2048,3072]{1,0:T(8,128)(2,1)} fusion(bf16[1002,3072]{1,0:T(8,128)(2,1)} %param.10, s32[2048]{0:T(1024)S(1)} %broadcast_clamp_fusion), kind=kCustom, calls=%fused_computation | custom fusion | bytes 25174016 | tf_op jit(solution)/shard_map/jit(_take)/gather | solution.py:76
  70.1 10.9 %select_select_fusion = bf16[32,64,3072]{2,1,0:T(8,128)(2,1)} fusion(bf16[32,64,3072]{2,1,0:T(8,128)(2,1)} %bitcast.63, pred[32,64]{1,0:T(8,128)(4,1)S(1)} %get-tuple-element.14, pred[32,64]{1,0:T(8,128)(4,1)S(1)} %and_bitcast_fusion), kind=kLoop, calls=%fused_computation.2 | loop fusion | flops 12582912 | bytes 25169920 | tf_op jit(solution)/shard_map/jit(_where)/select_n | solution.py:77
  81.1 0.7 all-gather.6.cloned.1.call-update
  84.5 42.8 %all-reduce.2 = (bf16[3072]{0:T(1024)(128)(2,1)S(1)}, bf16[3072]{0:T(1024)(128)(2,1)S(1)}) all-reduce(bf16[3072]{0:T(1024)(128)(2,1)S(1)} %dynamic-update-slice, bf16[3072]{0:T(1024)(128)(2,1)S(1)} %dynamic-update-slice.1), channel_id=1, replica_groups=mesh['dp'=1,'fsdp'=32] {'fsdp'}, use_global_device_ids=true, to_apply=%add | all-reduce | flops 6144 | bytes 24576
  127.5 48.9 %reduce-scatter.2.cloned.1.call-done = bf16[1,64,3072]{2,1,0:T(8,128)(2,1)} async-done(((bf16[32,64,3072]{2,1,0:T(8,128)(2,1)}), bf16[1,64,3072]{2,1,0:T(8,128)(2,1)}) %reduce-scatter.2.cloned.1.call-update) | async-done | bytes 393232 | tf_op jit(solution)/shard_map/reduce_scatter | solution.py:78
  176.3 1.2 fusion.12
  177.5 168.8 %all-gather.6.cloned.1.call-done = bf16[3072,9216]{1,0:T(8,128)(2,1)} async-done(((bf16[96,9216]{1,0:T(8,128)(2,1)}), bf16[3072,9216]{1,0:T(8,128)(2,1)}) %all-gather.6.cloned.1.call-update) | async-done | bytes 56623120 | tf_op jit(solution)/shard_map/all_gather | solution.py:64
  346.3 21.1 %convolution_bitcast_fusion.1 = f32[1,64,9216]{2,1,0:T(8,128)S(1)} fusion(bf16[3072,9216]{1,0:T(8,128)(2,1)} %all-gather.6.cloned.1.call-done, bf16[1,64,3072]{2,1,0:T(8,128)(2,1)} %reduce-scatter.2.cloned.1.call-done, f32[3072]{0:T(1024)S(1)} %convert_element_type.75, f32[64]{0:T(128)S(1)} %add_rsqrt_fusion.1), kind=kOutput, calls=%fused_computation.3 | convolution fusion | flops 3624665088 | bytes 59388160 | tf_op jit(solution)/shard_map/bld,de->ble/dot_general | solution.py:40
  367.5 1.3 convert_element_type.78
  368.8 1.3 convert_element_type.89
  370.1 1.0 fusion.38
  371.1 1.5 reshape.200
  373.1 0.7 fusion.39
  373.9 2.5 fusion.15
  376.6 1.1 copy.35
  377.8 0.7 fusion.41
  378.7 1.5 fusion.8
  381.3 38.3 %all-gather.8.cloned.1.call-done = bf16[3072,3072]{1,0:T(8,128)(2,1)} async-done(((bf16[96,3072]{1,0:T(8,128)(2,1)}), bf16[3072,3072]{1,0:T(8,128)(2,1)}) %all-gather.8.cloned.1.call-update) | async-done | bytes 18874384 | tf_op jit(solution)/shard_map/all_gather | solution.py:64
  419.6 8.2 multiply_reduce_fusion
  427.9 276.3 %all-gather.10.cloned.1.call-done = bf16[3072,16384]{1,0:T(8,128)(2,1)} async-done(((bf16[96,16384]{1,0:T(8,128)(2,1)}), bf16[3072,16384]{1,0:T(8,128)(2,1)}) %all-gather.10.cloned.1.call-update) | async-done | bytes 100663312 | tf_op jit(solution)/shard_map/all_gather | solution.py:64
  704.2 36.7 %convolution_bitcast_fusion = f32[1,64,16384]{2,1,0:T(8,128)} fusion(bf16[3072,16384]{1,0:T(8,128)(2,1)} %all-gather.10.cloned.1.call-done, f32[1,64,3072]{2,1,0:T(8,128)S(1)} %get-tuple-element.33, f32[3072]{0:T(1024)S(1)} %convert_element_type.85, f32[64]{0:T(128)S(1)} %add_rsqrt_fusion), kind=kOutput, calls=%fused_computation.1 | convolution fusion | flops 6443040768 | bytes 105656576 | tf_op jit(solution)/shard_map/bld,df->blf/dot_general | solution.py:56
  740.9 116.4 %all-gather.12.cloned.1.call-done = bf16[8192,3072]{1,0:T(8,128)(2,1)} async-done(((bf16[256,3072]{1,0:T(8,128)(2,1)}), bf16[8192,3072]{1,0:T(8,128)(2,1)}) %all-gather.12.cloned.1.call-update) | async-done | bytes 50331664 | tf_op jit(solution)/shard_map/all_gather | solution.py:64
  857.3 20.6 %fusion.4 = bf16[1,64,3072]{2,1,0:T(8,128)(2,1)} fusion(f32[1,64,3072]{2,1,0:T(8,128)S(1)} %get-tuple-element.33, bf16[8192,3072]{1,0:T(8,128)(2,1)} %all-gather.12.cloned.1.call-done, f32[1,64,16384]{2,1,0:T(8,128)} %convolution_bitcast_fusion), kind=kOutput, calls=%fused_computation.10 | convolution fusion | flops 3224764416 | bytes 55705600 | tf_op jit(solution)/shard_map/blf,fd->bld/dot_general | solution.py:58
  (38 shorter events, 5.1 us)
Async XLA Ops:
  7.2 169.1 %reduce-scatter.2.cloned.1.call-start = ((), (), s32[]{:S(2)}) async-start(), calls=%async_computation.1 | async-start | bytes 12976128 | tf_op jit(solution)/shard_map/reduce_scatter | solution.py:78
  81.0 3.0 copy-start.1
  81.0 3.2 copy-start.2
  81.0 46.3 %copy-start.3 = (f32[48]{0:T(128)S(1)}, f32[48]{0:T(128)}, u32[]{:S(2)}) copy-start(f32[48]{0:T(128)} %param.17) | copy-start | bytes 580
  81.1 265.2 %all-gather.6.cloned.1.call-start = ((), (), s32[]{:S(2)}) async-start(), calls=%async_computation.2 | async-start | bytes 58392576 | tf_op jit(solution)/shard_map/all_gather | solution.py:64
  81.9 337.8 %all-gather.8.cloned.1.call-start = ((), (), s32[]{:S(2)}) async-start(), calls=%async_computation.3 | async-start | bytes 19464192 | tf_op jit(solution)/shard_map/all_gather | solution.py:64
  82.7 621.5 %all-gather.10.cloned.1.call-start = ((), (), s32[]{:S(2)}) async-start(), calls=%async_computation.4 | async-start | bytes 103809024 | tf_op jit(solution)/shard_map/all_gather | solution.py:64
  83.3 774.0 %all-gather.12.cloned.1.call-start = ((), (), s32[]{:S(2)}) async-start(), calls=%async_computation.5 | async-start | bytes 51904512 | tf_op jit(solution)/shard_map/all_gather | solution.py:64
  373.1 46.5 %copy-start = (bf16[1,64,3072]{2,1,0:T(8,128)(2,1)S(1)}, bf16[1,64,3072]{2,1,0:T(8,128)(2,1)}, u32[]{:S(2)}) copy-start(bf16[1,64,3072]{2,1,0:T(8,128)(2,1)} %reduce-scatter.2.cloned.1.call-done) | copy-start | bytes 1179652
Sparse Core Ops, SparseCore 0:
  81.2 95.0 reduce-scatter.1
  178.4 167.8 all-gather.5
  348.4 71.2 all-gather.7
  421.6 282.5 all-gather.9
  706.1 151.1 all-gather.11
where the time goes:
time: 887 us; the launch traced here: 884 us
  waiting for transfers between devices  651 us (73%)
  matrix products  88.9 us (10%)
  blocking collectives  79 us (9%)
  local copies, waits for them, and re-layouts  35.7 us (4%)
  other arithmetic  15.3 us (2%)
  between operations  14 us (2%)
    all_gather x4, waiting for transfers between devices, gather_rows(): return lax.all_gather(weight, 'fsdp', axis=0, tiled=True)  600 us
    reduce_scatter x1, waiting for transfers between devices, device_step(): lax.psum_scatter(table_rows, 'fsdp', scatter_dimension=0, tiled=True)  48.9 us
    unnamed x1, blocking collectives  42.8 us
    dot_general x1, matrix products, decoder_layer(): jnp.einsum('bld,df->blf', normed_mlp, w_gate_up, preferred_element_type=j...  36.7 us
    all_gather x1, blocking collectives, device_step(): group_tokens = lax.all_gather(tokens, 'fsdp', axis=0, tiled=True)  36.2 us
    gather x1, local copies, waits for them, and re-layouts, device_step(): jnp.take(embed_table, jnp.clip(local_ids, 0, shard_rows - 1), axis=0)  26.5 us
    dot_general x1, matrix products, decoder_layer(): jnp.einsum('bld,de->ble', normed, w_qkv, preferred_element_type=jnp.float32)  21.1 us
    dot_general x1, matrix products, decoder_layer(): jnp.einsum('blf,fd->bld', mlp_act, w_down, preferred_element_type=jnp.flo...  20.6 us
  transfers between devices with their start and end apart: 5, of which 5 were waited for; matrix products, arithmetic and copies ran while one was open for 9% of the time, Pallas kernels for 0%

commit v1 on v0

v1 whole, which is shorter than its diff:
```python
import functools
import math

import jax
import jax.numpy as jnp
from jax import lax
from jax.experimental import pallas as pl
from jax.experimental.pallas import tpu as pltpu
from jax.sharding import PartitionSpec as P

NORM_EPS = 1e-5
ROPE_THETA = 10000.0
AXIS = 'fsdp'
MESH = pl.DeviceIdType.MESH
ANY = pl.BlockSpec(memory_space=pl.ANY)
VMEM_LIMIT = 60 * 1024 * 1024


class Place:
    def __init__(self, side):
        me = lax.axis_index(AXIS)
        self.side = side
        self.c = lax.rem(me, 2)
        chip = lax.div(me, 2)
        self.y = lax.div(chip, side)
        self.x = lax.rem(chip, side)
        self.me = me
        self.partner = me + 1 - 2 * self.c

    def chip(self, dy, dx):
        s = self.side
        return lax.rem(self.y + dy + s, s) * s + lax.rem(self.x + dx + s, s)

    def dev(self, dy, dx):
        return self.chip(dy, dx) * 2 + self.c


def barrier(devices):
    sem = pltpu.get_barrier_semaphore()
    for d in devices:
        pl.semaphore_signal(sem, inc=1, device_id={AXIS: d}, device_id_type=MESH)
    pl.semaphore_wait(sem, len(devices))


class Msgs:
    def __init__(self, send_sem, recv_sem):
        self.send_sem, self.recv_sem = send_sem, recv_sem
        self.index, self.copies = {}, []

    def start(self, name, src, dst, dev):
        i = len(self.copies)
        self.index[name] = i
        copy = pltpu.make_async_remote_copy(
            src_ref=src, dst_ref=dst, send_sem=self.send_sem.at[i], recv_sem=self.recv_sem.at[i],
            device_id={AXIS: dev}, device_id_type=MESH)
        copy.start()
        self.copies.append(copy)

    def recv(self, name):
        self.copies[self.index[name]].wait_recv()

    def drain(self):
        for copy in self.copies:
            copy.wait_send()


AG_MSGS = 40
RS_MSGS = 40


def torus_all_gather(pos, m, blk, width):
    q = width // 4
    halves = (0, 1)
    order = (0, -1, 1, 2)

    def at(h, a, b):
        return (b, a) if h == 0 else (a, b)

    def chip(h, a, b):
        return pos.chip(*at(h, a, b))

    def dev(h, a, b):
        return pos.dev(*at(h, a, b))

    def send(h, name, a, b, lo, n, ta, tb):
        ref = blk(chip(h, a, b), 2 * q * h + lo, n)
        m.start(('ag', h) + name, ref, ref, dev(h, ta, tb))

    def recv(h, *name):
        m.recv(('ag', h) + name)

    def second(h, a):
        send(h, ('2p', a), a, 0, 0, 2 * q, 0, 1)
        send(h, ('2m', a), a, 0, 0, 2 * q, 0, -1)

    def second_forward(h, a):
        recv(h, '2p', a)
        send(h, ('2pf', a), a, -1, 0, q, 0, 1)
        recv(h, '2m', a)
        send(h, ('2mf', a), a, 1, q, q, 0, -1)

    for h in halves:
        send(h, ('1p',), 0, 0, 0, 2 * q, 1, 0)
        send(h, ('1m',), 0, 0, 0, 2 * q, -1, 0)
    for h in halves:
        second(h, 0)
    for h in halves:
        recv(h, '1p')
        send(h, ('1pf',), -1, 0, 0, q, 1, 0)
        second(h, -1)
    for h in halves:
        recv(h, '1m')
        send(h, ('1mf',), 1, 0, q, q, -1, 0)
        second(h, 1)
    for h in halves:
        second_forward(h, 0)
    for h in halves:
        recv(h, '1pf')
        recv(h, '1mf')
        second(h, 2)
    for a in (-1, 1, 2):
        for h in halves:
            second_forward(h, a)
    for a in order:
        for h in halves:
            recv(h, '2pf', a)
            recv(h, '2mf', a)


def torus_reduce_scatter(pos, m, part, recv_buf, width):
    q = width // 4
    halves = (0, 1)
    slots = {}

    def at(h, a, b):
        return (a, b) if h == 0 else (b, a)

    def chip(h, a, b):
        return pos.chip(*at(h, a, b))

    def dev(h, a, b):
        return pos.dev(*at(h, a, b))

    def slot(key, n):
        if key not in slots:
            slots[key] = sum(k for _, k in slots.values()), n
        return slots[key][0]

    def send(h, name, a, b, lo, n, ta, tb):
        key = ('rs', h) + name
        first = slot(key, n // q)
        src = part.at[chip(h, a, b), :, pl.ds(2 * q * h + lo, n)]
        m.start(key, src, recv_buf.at[:, pl.ds(first * q, n)], dev(h, ta, tb))

    def recv_add(h, name, a, b, lo, n):
        key = ('rs', h) + name
        m.recv(key)
        first = slots[key][0]
        sl = pl.ds(2 * q * h + lo, n)
        p = chip(h, a, b)
        part[p, :, sl] = part[p, :, sl] + recv_buf[:, pl.ds(first * q, n)]

    order = (2, 1, -1, 0)
    for b in order:
        for h in halves:
            send(h, ('1pf', b), 2, b, 0, q, 1, 0)
            send(h, ('1mf', b), 2, b, q, q, -1, 0)
    for b in order:
        for h in halves:
            recv_add(h, ('1pf', b), 1, b, 0, q)
            send(h, ('1p', b), 1, b, 0, 2 * q, 1, 0)
            recv_add(h, ('1mf', b), -1, b, q, q)
            send(h, ('1m', b), -1, b, 0, 2 * q, -1, 0)
    for b in order:
        for h in halves:
            recv_add(h, ('1p', b), 0, b, 0, 2 * q)
            recv_add(h, ('1m', b), 0, b, 0, 2 * q)
            if b == 2:
                send(h, ('2pf',), 0, 2, 0, q, 0, 1)
                send(h, ('2mf',), 0, 2, q, q, 0, -1)
            if b == 1:
                recv_add(h, ('2pf',), 0, 1, 0, q)
                send(h, ('2p',), 0, 1, 0, 2 * q, 0, 1)
            if b == -1:
                recv_add(h, ('2mf',), 0, -1, q, q)
                send(h, ('2m',), 0, -1, 0, 2 * q, 0, -1)
            if b == 0:
                recv_add(h, ('2p',), 0, 0, 0, 2 * q)
                recv_add(h, ('2m',), 0, 0, 0, 2 * q)


def torus_neighbours(pos):
    return [pos.dev(0, 1), pos.dev(0, -1), pos.dev(1, 0), pos.dev(-1, 0)]


def offsets(side):
    every = [(dy, dx) for dy in range(side) for dx in range(side) if (dy, dx) != (0, 0)]
    return sorted(every, key=lambda o: min(o[0], side - o[0]) + min(o[1], side - o[1]))


def start_kernel(side, tok, wq, wgu, wo, table, tok_all, wq_all, wgu_all, wo_all, table_other,
                 t_send, t_recv, q_send, q_recv, g_send, g_recv, o_send, o_recv, f_send, f_recv, l_sem):
    pos = Place(side)
    offs = offsets(side)
    me_chip = pos.chip(0, 0)
    ff = wgu.shape[1] // 2
    ffb = ff // (side * side)
    barrier([pos.dev(dy, dx) for dy, dx in offs] + [pos.partner])

    def remote(src, dst, s, r, dev):
        return pltpu.make_async_remote_copy(src_ref=src, dst_ref=dst, send_sem=s, recv_sem=r,
                                            device_id={AXIS: dev}, device_id_type=MESH)

    toks, qs, gs, fs = [], [], [], []
    for i, (dy, dx) in enumerate(offs):
        cp = remote(tok, tok_all.at[me_chip], t_send.at[i], t_recv.at[i], pos.dev(dy, dx))
        cp.start()
        toks.append(cp)
    tcp = remote(table, table_other, f_send.at[0], f_recv.at[0], pos.partner)
    tcp.start()
    for i, (dy, dx) in enumerate(offs):
        cp = remote(wq.at[pos.chip(dy, dx)], wq_all.at[me_chip, pos.c], q_send.at[i], q_recv.at[i], pos.dev(dy, dx))
        cp.start()
        qs.append(cp)
    own = [pltpu.make_async_copy(tok, tok_all.at[me_chip], l_sem.at[0]),
           pltpu.make_async_copy(wq.at[me_chip], wq_all.at[me_chip, pos.c], l_sem.at[1]),
           pltpu.make_async_copy(wo, wo_all.at[me_chip, pos.c], l_sem.at[2])]
    for j in (0, 1):
        src = wgu.at[:, pl.ds(pl.multiple_of(j * ff + me_chip * ffb, 128), ffb)]
        own.append(pltpu.make_async_copy(src, wgu_all.at[me_chip, pos.c, :, pl.ds(j * ffb, ffb)], l_sem.at[3 + j]))
    for cp in own:
        cp.start()
    for i, (dy, dx) in enumerate(offs):
        for j in (0, 1):
            src = wgu.at[:, pl.ds(pl.multiple_of(j * ff + pos.chip(dy, dx) * ffb, 128), ffb)]
            cp = remote(src, wgu_all.at[me_chip, pos.c, :, pl.ds(j * ffb, ffb)],
                        g_send.at[2 * i + j], g_recv.at[2 * i + j], pos.dev(dy, dx))
            cp.start()
            gs.append(cp)
    for cp in own:
        cp.wait()

    def forward(k, ref):
        cp = remote(ref, ref, f_send.at[k], f_recv.at[k], pos.partner)
        cp.start()
        fs.append(cp)

    forward(1, wq_all.at[me_chip, pos.c])
    forward(2, wgu_all.at[me_chip, pos.c])
    forward(3, wo_all.at[me_chip, pos.c])
    for i, (dy, dx) in enumerate(offs):
        qs[i].wait_recv()
        forward(4 + i, wq_all.at[pos.chip(-dy, -dx), pos.c])
    m = Msgs(o_send, o_recv)
    torus_all_gather(pos, m, lambda p, lo, n: wo_all.at[p, pos.c, :, pl.ds(lo, n)], wo.shape[1])
    n = len(offs)
    for i, (dy, dx) in enumerate(offs):
        forward(4 + n + i, wo_all.at[pos.chip(-dy, -dx), pos.c])
    for i, (dy, dx) in enumerate(offs):
        gs[2 * i].wait_recv()
        gs[2 * i + 1].wait_recv()
        forward(4 + 2 * n + i, wgu_all.at[pos.chip(-dy, -dx), pos.c])
    for cp in toks:
        cp.wait()
    tcp.wait()
    for cp in qs + gs:
        cp.wait_send()
    m.drain()
    for cp in fs:
        cp.wait()


def embed_kernel(side, part_hbm, x_all, part, recv_buf, s1, r1, s2, r2, l_sem):
    pos = Place(side)
    barrier(torus_neighbours(pos))
    width = x_all.shape[2]
    loads = [pltpu.make_async_copy(part_hbm.at[i], part.at[i], l_sem.at[i]) for i in range(side * side)]
    for cp in loads:
        cp.start()
    for cp in loads:
        cp.wait()
    m = Msgs(s1, r1)
    torus_reduce_scatter(pos, m, part, recv_buf, width)
    me_chip = pos.chip(0, 0)
    x_all[me_chip] = part[me_chip]
    m2 = Msgs(s2, r2)
    torus_all_gather(pos, m2, lambda p, lo, n: x_all.at[p, :, pl.ds(lo, n)], width)
    m.drain()
    m2.drain()


def gather_kernel(side, x, x_all, s2, r2, l_sem):
    pos = Place(side)
    me_chip = pos.chip(0, 0)
    cp = pltpu.make_async_copy(x, x_all.at[me_chip], l_sem.at[0])
    cp.start()
    barrier(torus_neighbours(pos))
    cp.wait()
    m = Msgs(s2, r2)
    torus_all_gather(pos, m, lambda p, lo, n: x_all.at[p, :, pl.ds(lo, n)], x_all.shape[2])
    m.drain()


def scatter_kernel(side, part_hbm, out, part, recv_buf, s1, r1, l_sem):
    pos = Place(side)
    barrier(torus_neighbours(pos))
    width = out.shape[1]
    loads = [pltpu.make_async_copy(part_hbm.at[i], part.at[i], l_sem.at[i]) for i in range(side * side)]
    for cp in loads:
        cp.start()
    for cp in loads:
        cp.wait()
    m = Msgs(s1, r1)
    torus_reduce_scatter(pos, m, part, recv_buf, width)
    out[...] = part[pos.chip(0, 0)]
    m.drain()


def exchange_kernel(side, src, dst, sems, recvs, l_sem):
    pos = Place(side)
    offs = offsets(side)
    me_chip = pos.chip(0, 0)
    barrier([pos.dev(dy, dx) for dy, dx in offs])
    copies = []
    for i, (dy, dx) in enumerate(offs):
        cp = pltpu.make_async_remote_copy(
            src_ref=src.at[pos.chip(dy, dx)], dst_ref=dst.at[me_chip], send_sem=sems.at[i], recv_sem=recvs.at[i],
            device_id={AXIS: pos.dev(dy, dx)}, device_id_type=MESH)
        cp.start()
        copies.append(cp)
    own = pltpu.make_async_copy(src.at[me_chip], dst.at[me_chip], l_sem.at[0])
    own.start()
    own.wait()
    for cp in copies:
        cp.wait()


def dma(n):
    return pltpu.SemaphoreType.DMA((n,))


def params(cid):
    return pltpu.CompilerParams(collective_id=cid, has_side_effects=True, vmem_limit_bytes=VMEM_LIMIT)


def rms_norm(hidden, gain):
    h_f32 = hidden.astype(jnp.float32)
    inv_rms = lax.rsqrt(jnp.mean(h_f32 * h_f32, axis=-1, keepdims=True) + NORM_EPS)
    return (h_f32 * inv_rms * gain.astype(jnp.float32)).astype(jnp.bfloat16)


def apply_rope(proj, rope_scale):
    seq_len = proj.shape[1]
    head_dim = proj.shape[-1]
    half_dim = head_dim // 2
    freq_expo = jnp.arange(half_dim, dtype=jnp.float32) * (2.0 / head_dim)
    inv_freq = 1.0 / (rope_scale * jnp.power(ROPE_THETA, freq_expo))
    angles = jnp.arange(seq_len, dtype=jnp.float32)[:, None] * inv_freq[None, :]
    cos_tab = jnp.cos(angles)[:, None, :]
    sin_tab = jnp.sin(angles)[:, None, :]
    low_half = proj[..., :half_dim]
    high_half = proj[..., half_dim:]
    return jnp.concatenate([low_half * cos_tab - high_half * sin_tab, high_half * cos_tab + low_half * sin_tab], axis=-1)


def solution(mesh):
    batch_axes = ('dp', AXIS)
    row_spec = P(AXIS, None)
    n_dev = mesh.shape[AXIS]
    chips = n_dev // 2
    side = math.isqrt(chips)
    n_off = chips - 1

    def device_step(tokens, embed_table, norm_attn, w_qkv, w_out, norm_mlp, w_gate_up, w_down, rope_scale):
        f32, bf16 = jnp.float32, jnp.bfloat16
        seq = tokens.shape[1]
        rows, d_model = w_out.shape
        rows_table = embed_table.shape[0]
        head_dim = 2 * rope_scale.shape[0]
        q_width = rows * n_dev
        kv_width = (w_qkv.shape[1] - q_width) // 2
        heads = q_width // head_dim // chips
        kv_heads = kv_width // head_dim // chips
        qb, kb = heads * head_dim, kv_heads * head_dim
        width = qb + 2 * kb
        pad_width = -(-(width + 2) // 128) * 128
        ff = w_gate_up.shape[1] // 2
        ffb = ff // chips
        me = lax.axis_index(AXIS)
        rest = jnp.zeros((chips, rows, pad_width - width - 2), bf16)
        wq_blocks = jnp.concatenate([
            w_qkv[:, :q_width].reshape(rows, chips, qb).transpose(1, 0, 2),
            w_qkv[:, q_width:q_width + kv_width].reshape(rows, chips, kb).transpose(1, 0, 2),
            w_qkv[:, q_width + kv_width:].reshape(rows, chips, kb).transpose(1, 0, 2),
            jnp.broadcast_to(norm_attn[None, :, None], (chips, rows, 1)),
            jnp.broadcast_to(norm_mlp[None, :, None], (chips, rows, 1)), rest], axis=-1)

        tok_all, wq_all, wgu_all, wo_all, table_other = pl.pallas_call(
            functools.partial(start_kernel, side), name='start',
            out_shape=(jax.ShapeDtypeStruct((chips, 1, seq), jnp.int32),
                       jax.ShapeDtypeStruct((chips, 2, rows, pad_width), bf16),
                       jax.ShapeDtypeStruct((chips, 2, rows, 2 * ffb), bf16),
                       jax.ShapeDtypeStruct((chips, 2, rows, d_model), bf16),
                       jax.ShapeDtypeStruct((rows_table, d_model), bf16)),
            in_specs=[ANY] * 5, out_specs=(ANY,) * 5,
            scratch_shapes=[dma(n_off), dma(n_off), dma(n_off), dma(n_off), dma(2 * n_off), dma(2 * n_off),
                            dma(AG_MSGS), dma(AG_MSGS), dma(4 + 3 * n_off), dma(4 + 3 * n_off), dma(5)],
            compiler_params=params(1),
        )(tokens, wq_blocks, w_gate_up, w_out, embed_table)

        gains = wq_all[..., width:width + 2].reshape(d_model, 2)
        gain_attn, gain_mlp = gains[:, 0], gains[:, 1]
        wq_own = wq_all.reshape(d_model, pad_width)
        wgu_own = wgu_all.reshape(d_model, 2 * ffb)
        wo_full = wo_all.reshape(q_width, d_model)

        ids = tok_all.reshape(chips * seq)
        row_ids = jnp.arange(rows_table, dtype=jnp.int32)

        def pick(device, table):
            hot = ((ids - device * rows_table)[:, None] == row_ids[None, :]).astype(bf16)
            return jnp.dot(hot, table, preferred_element_type=f32)

        part = (pick(me, embed_table) + pick(me + 1 - 2 * lax.rem(me, 2), table_other)).astype(bf16)
        part = part.reshape(chips, seq, d_model)

        x_all = pl.pallas_call(
            functools.partial(embed_kernel, side), name='embed',
            out_shape=jax.ShapeDtypeStruct((chips, seq, d_model), bf16),
            in_specs=[ANY], out_specs=pl.BlockSpec(memory_space=pltpu.VMEM),
            scratch_shapes=[pltpu.VMEM((chips, seq, d_model), bf16),
                            pltpu.VMEM((seq, d_model * n_off), bf16),
                            dma(RS_MSGS), dma(RS_MSGS), dma(AG_MSGS), dma(AG_MSGS), dma(chips)],
            compiler_params=params(2),
        )(part)
        chip = lax.div(me, 2)
        x_own = lax.dynamic_index_in_dim(x_all, chip, 0, keepdims=False)

        normed = rms_norm(x_all.reshape(chips * seq, d_model), gain_attn)
        proj = jnp.dot(normed, wq_own, preferred_element_type=f32)[:, :width].reshape(chips, seq, width)
        query = apply_rope(proj[..., :qb].reshape(chips, seq, heads, head_dim), rope_scale).astype(bf16)
        key = apply_rope(proj[..., qb:qb + kb].reshape(chips, seq, kv_heads, head_dim), rope_scale).astype(bf16)
        value = proj[..., qb + kb:].astype(bf16).reshape(chips, seq, kv_heads, head_dim)
        q_grouped = query.reshape(chips, seq, kv_heads, heads // kv_heads, head_dim)
        scores = jnp.einsum('bqkgd,bskd->bkgqs', q_grouped, key, preferred_element_type=f32) * (head_dim ** -0.5)
        causal = jnp.arange(seq)[:, None] >= jnp.arange(seq)[None, :]
        scores = jnp.where(causal, scores, -jnp.inf)
        scores = scores - jnp.max(scores, axis=-1, keepdims=True)
        weights = jnp.exp(scores)
        probs = (weights / jnp.sum(weights, axis=-1, keepdims=True)).astype(bf16)
        context = jnp.einsum('bkgqs,bskd->bqkgd', probs, value, preferred_element_type=f32).astype(bf16)
        context = context.reshape(chips, seq, qb)
        packed = jnp.concatenate([context, key.reshape(chips, seq, kb), value.reshape(chips, seq, kb)], axis=-1)

        mine = pl.pallas_call(
            functools.partial(exchange_kernel, side), name='to_sequences',
            out_shape=jax.ShapeDtypeStruct((chips, seq, width), bf16),
            in_specs=[ANY], out_specs=ANY,
            scratch_shapes=[dma(n_off), dma(n_off), dma(1)],
            compiler_params=params(3),
        )(packed)
        ctx_own = mine[..., :qb].transpose(1, 0, 2).reshape(seq, q_width)
        key_own = mine[..., qb:qb + kb].reshape(chips, seq, kv_heads, head_dim).transpose(1, 0, 2, 3)
        val_own = mine[..., qb + kb:].reshape(chips, seq, kv_heads, head_dim).transpose(1, 0, 2, 3)
        key_own = key_own.reshape(1, seq, chips * kv_heads, head_dim)
        val_own = val_own.reshape(1, seq, chips * kv_heads, head_dim)

        attn_proj = jnp.dot(ctx_own, wo_full, preferred_element_type=f32)
        x_mid = (x_own.astype(f32) + attn_proj).astype(bf16)
        normed_mlp = rms_norm(x_mid, gain_mlp)

        h_all = pl.pallas_call(
            functools.partial(gather_kernel, side), name='gather_hidden',
            out_shape=jax.ShapeDtypeStruct((chips, seq, d_model), bf16),
            in_specs=[pl.BlockSpec(memory_space=pltpu.VMEM)], out_specs=pl.BlockSpec(memory_space=pl.ANY),
            scratch_shapes=[dma(AG_MSGS), dma(AG_MSGS), dma(1)],
            compiler_params=params(4),
        )(normed_mlp)

        wd_other = pl.pallas_call(
            swap_kernel, name='swap_down',
            out_shape=jax.ShapeDtypeStruct(w_down.shape, bf16),
            in_specs=[ANY], out_specs=ANY, scratch_shapes=[dma(1), dma(1)],
            compiler_params=params(6),
        )(w_down)
        first = lax.rem(me, 2) == 0

        gate_up = jnp.dot(h_all.reshape(chips * seq, d_model), wgu_own, preferred_element_type=f32)
        act = (jax.nn.silu(gate_up[:, :ffb]) * gate_up[:, ffb:]).astype(bf16)
        half = ffb // 2
        act_own = lax.dynamic_slice_in_dim(act, lax.rem(me, 2) * half, half, axis=1)
        act_other = lax.dynamic_slice_in_dim(act, (1 - lax.rem(me, 2)) * half, half, axis=1)
        down = (jnp.dot(act_own, w_down, preferred_element_type=f32)
                + jnp.dot(act_other, wd_other, preferred_element_type=f32))

        total = pl.pallas_call(
            functools.partial(scatter_kernel, side), name='scatter_down',
            out_shape=jax.ShapeDtypeStruct((seq, d_model), f32),
            in_specs=[ANY], out_specs=pl.BlockSpec(memory_space=pltpu.VMEM),
            scratch_shapes=[pltpu.VMEM((chips, seq, d_model), f32),
                            pltpu.VMEM((seq, d_model * n_off), f32),
                            dma(RS_MSGS), dma(RS_MSGS), dma(chips)],
            compiler_params=params(5),
        )(down.reshape(chips, seq, d_model))
        layer_out = (x_mid.astype(f32) + total).astype(bf16)
        return layer_out[None], key_own, val_own

    return jax.shard_map(
        device_step,
        mesh=mesh,
        in_specs=(P(batch_axes, None), row_spec, P(AXIS), row_spec, row_spec, P(AXIS), row_spec, row_spec, P(None)),
        out_specs=(P(batch_axes, None, None), P(batch_axes, None, None, None), P(batch_axes, None, None, None)),
        check_vma=False,
    )


def swap_kernel(src, dst, send_sem, recv_sem):
    me = lax.axis_index(AXIS)
    partner = me + 1 - 2 * lax.rem(me, 2)
    barrier([partner])
    cp = pltpu.make_async_remote_copy(src_ref=src, dst_ref=dst, send_sem=send_sem.at[0], recv_sem=recv_sem.at[0],
                                      device_id={AXIS: partner}, device_id_type=MESH)
    cp.start()
    cp.wait()
```

time: 887 us -> 486 us (0.55)
  waiting for transfers between devices: 651 us -> 0 us
  Pallas kernels: 0 us -> 354 us
  blocking collectives: 79 us -> 0 us
  matrix products: 88.9 us -> 71.6 us
  between operations: 14 us -> 1.48 us
    all_gather x4 -> x0, waiting for transfers between devices: 600 us -> none  [gather_rows(): return lax.all_gather(weight, 'fsdp', axis=0, tiled=True)]
    pallas_call x0 -> x6, Pallas kernels: none -> 354 us  [the longest x1 137 us: device_step(): pl.pallas_call(functools.partial(start_kernel, side), name='start', out_s...]
    reduce_scatter x1 -> x0, waiting for transfers between devices: 48.9 us -> none  [device_step(): lax.psum_scatter(table_rows, 'fsdp', scatter_dimension=0, tiled=True)]
    unnamed x1 -> x0, blocking collectives: 42.8 us -> none
    all_gather x1 -> x0, blocking collectives: 36.2 us -> none  [device_step(): group_tokens = lax.all_gather(tokens, 'fsdp', axis=0, tiled=True)]
    gather x1 -> x0, local copies, waits for them, and re-layouts: 26.5 us -> none  [device_step(): jnp.take(embed_table, jnp.clip(local_ids, 0, shard_rows - 1), axis=0)]
    dot_general x6 -> x8, matrix products: 88.9 us -> 66.6 us  [the longest x2 26 us: pick(): return jnp.dot(hot, table, preferred_element_type=f32)]
    select_n x1 -> x0, other arithmetic: 10.9 us -> none  [device_step(): jnp.where(owned_mask[..., None], table_rows, jnp.zeros((), table_rows.dty...]
  transfers between devices with their start and end apart: 5 -> 0, of which waited for: 5 -> 0; matrix products, arithmetic and copies ran while one was open for 9% -> 0% of each run, Pallas kernels for 0% -> 0%
where the time goes in v1:
time: 486 us; the launch traced here: 483 us
  Pallas kernels  354 us (73%)
  matrix products  71.6 us (15%)
  local copies, waits for them, and re-layouts  35.6 us (7%)
  other arithmetic  20.2 us (4%)
    pallas_call x1, Pallas kernels, device_step(): pl.pallas_call(functools.partial(start_kernel, side), name='start', out_s...  137 us
    pallas_call x1, Pallas kernels, device_step(): pl.pallas_call(functools.partial(embed_kernel, side), name='embed', out_s...  81.1 us
    pallas_call x1, Pallas kernels, device_step(): pl.pallas_call(functools.partial(scatter_kernel, side), name='scatter_dow...  75.6 us
    pallas_call x1, Pallas kernels, device_step(): pl.pallas_call(functools.partial(gather_kernel, side), name='gather_hidde...  35.5 us
    dot_general x2, matrix products, pick(): return jnp.dot(hot, table, preferred_element_type=f32)  26 us
    pallas_call x1, Pallas kernels, device_step(): pl.pallas_call(functools.partial(exchange_kernel, side), name='to_sequenc...  22.1 us
    dot_general x1, matrix products, device_step(): jnp.dot(act_other, wd_other, preferred_element_type=f32)  11.6 us
    dot_general x1, matrix products, device_step(): jnp.dot(h_all.reshape(chips * seq, d_model), wgu_own, preferred_element_t...  10.6 us

profile of v1, /device:TPU:96, one launch (start us, length us, event | category | flops | bytes accessed | tf_op | source)
XLA Modules:
  0.0 483.3 jit_solution(8842514703899447452)
XLA Ops:
  0.6 2.4 fusion.31
  5.3 2.4 reshape.201
  8.3 3.2 concatenate.15.wq
  11.5 136.7 %start.1 = (s32[16,1,64]{2,1,0:T(1,128)}, bf16[16,2,96,640]{3,2,1,0:T(8,128)(2,1)}, bf16[16,2,96,1024]{3,2,1,0:T(8,128)(2,1)}, bf16[16,2,96,3072]{3,2,1,0:T(8,128)(2,1)}, bf16[1002,3072]{1,0:T(8,128)(2,1)}) custom-call(s32[1,64]{1,0:T(1,128)} %tok.1, bf16[16,96,640]{2,1,0:T(8,128)(2,1)} %concatenate.15.wq, bf16[96,16384]{1,0:T(8,128)(2,1)} %wgu.1, ...), custom_call_target="tpu_custom_call" | custom-call | tf_op jit(solution)/shard_map/start/pallas_call | solution.py:398
  149.1 12.5 %fusion.3 = f32[1024,3072]{1,0:T(8,128)} fusion(bf16[1002,3072]{1,0:T(8,128)(2,1)} %table.1, s32[1024]{0:T(1024)S(1)} %sub.48), kind=kOutput, calls=%fused_computation.9 | convolution fusion | flops 6305064960 | bytes 18743296 | tf_op jit(solution)/shard_map/dot_general | solution.py:422
  161.6 13.5 %add_convert_fusion = bf16[1024,3072]{1,0:T(8,128)(2,1)} fusion(f32[1024,3072]{1,0:T(8,128)} %fusion.3, bf16[1002,3072]{1,0:T(8,128)(2,1)} %get-tuple-element.9, s32[1024]{0:T(1024)S(1)} %sub.52), kind=kOutput, calls=%fused_computation.5 | convolution fusion | flops 6311356416 | bytes 25034752 | tf_op jit(solution)/shard_map/dot_general | solution.py:422
  175.1 81.1 %embed.1 = bf16[16,64,3072]{2,1,0:T(8,128)(2,1)} custom-call(bf16[16,64,3072]{2,1,0:T(8,128)(2,1)} %bitcast.57), custom_call_target="tpu_custom_call" | custom-call | tf_op jit(solution)/shard_map/embed/pallas_call | solution.py:427
  256.2 4.1 fusion
  265.1 5.5 %fusion.2 = bf16[16,64,3072]{2,1,0:T(8,128)(2,1)S(1)} fusion(bf16[16,64,3072]{2,1,0:T(8,128)(2,1)} %embed.1, f32[3072]{0:T(1024)S(1)} %bitcast.68, f32[16,64]{1,0:T(8,128)S(1)} %add_rsqrt_fusion), kind=kLoop, calls=%fused_computation.4 | loop fusion | flops 12582912 | bytes 12599296 | tf_op jit(solution)/shard_map/convert_element_type | solution.py:349
  270.6 5.0 %fusion.4 = f32[1024,576]{1,0:T(8,128)S(1)} fusion(bf16[1024,3072]{1,0:T(8,128)(2,1)S(1)} %bitcast.58, bf16[3072,640]{1,0:T(8,128)(2,1)S(1)} %bitcast.67), kind=kOutput, calls=%fused_computation.10 | convolution fusion | flops 3623878656 | bytes 12582912 | tf_op jit(solution)/shard_map/slice | solution.py:440
  275.6 1.9 fusion.30
  277.8 1.9 reshape.210
  282.4 1.9 reshape.209
  293.6 2.7 pad_maximum_fusion.src
  296.3 22.1 %to_sequences.1 = bf16[16,64,576]{2,1,0:T(8,128)(2,1)} custom-call(bf16[16,64,576]{2,1,0:T(8,128)(2,1)} %pad_maximum_fusion.src), custom_call_target="tpu_custom_call" | custom-call | tf_op jit(solution)/shard_map/to_sequences/pallas_call | solution.py:455
  318.4 2.7 fusion.32
  322.0 9.9 %multiply_reduce_fusion = (f32[64]{0:T(128)S(1)}, f32[64,3072]{1,0:T(8,128)S(1)}) fusion(bf16[64,3072]{1,0:T(8,128)(2,1)S(1)} %reshape.213, bf16[3072,3072]{1,0:T(8,128)(2,1)} %bitcast.55, bf16[16,64,3072]{2,1,0:T(8,128)(2,1)} %embed.1, s32[]{:T(128)S(6)} %select_n.14), kind=kOutput, calls=%fused_computation.41 | convolution fusion | flops 1209139200 | bytes 20447492 | tf_op jit(solution)/shard_map/dot_general | solution.py:468
  333.5 35.5 %gather_hidden.1 = bf16[16,64,3072]{2,1,0:T(8,128)(2,1)} custom-call(bf16[64,3072]{1,0:T(8,128)(2,1)} %multiply_convert_fusion.x), custom_call_target="tpu_custom_call" | custom-call | tf_op jit(solution)/shard_map/gather_hidden/pallas_call | solution.py:472
  369.1 10.6 %fusion.36 = f32[1024,1024]{1,0:T(8,128)S(1)} fusion(bf16[1024,3072]{1,0:T(8,128)(2,1)} %bitcast.59, bf16[3072,1024]{1,0:T(8,128)(2,1)} %bitcast.70), kind=kOutput, calls=%fused_computation.71 | convolution fusion | flops 6442450944 | bytes 16777216 | tf_op jit(solution)/shard_map/dot_general | solution.py:488
  381.1 6.3 %fusion.21 = f32[1024,3072]{1,0:T(8,128)} fusion(bf16[256,3072]{1,0:T(8,128)(2,1)S(1)} %copy-done, bf16[1024,512]{1,0:T(8,128)(2,1)S(1)} %fusion.8, s32[]{:T(128)S(6)} %select_n.16), kind=kOutput, calls=%fused_computation.48 | convolution fusion | flops 1610612736 | bytes 14680068 | tf_op jit(solution)/shard_map/dot_general | solution.py:493
  387.4 3.4 swap_down.1
  390.8 11.6 %convolution_add_fusion = f32[1024,3072]{1,0:T(8,128)} fusion(f32[1024,3072]{1,0:T(8,128)} %fusion.21, bf16[256,3072]{1,0:T(8,128)(2,1)} %swap_down.1, bf16[1024,512]{1,0:T(8,128)(2,1)S(1)} %fusion.8, s32[]{:T(128)S(6)} %select_n.17), kind=kOutput, calls=%fused_computation.6 | convolution fusion | flops 1613758464 | bytes 27262980 | tf_op jit(solution)/shard_map/dot_general | solution.py:494
  402.4 75.6 %scatter_down.1 = f32[64,3072]{1,0:T(8,128)} custom-call(f32[16,64,3072]{2,1,0:T(8,128)} %bitcast.54), custom_call_target="tpu_custom_call" | custom-call | tf_op jit(solution)/shard_map/scatter_down/pallas_call | solution.py:496
  478.0 2.0 fusion.24
  (61 shorter events, 27.3 us)
Async XLA Ops:
  3.0 5.0 %copy-start.7 = (bf16[96]{0:T(256)(128)(2,1)S(1)}, bf16[96]{0:T(256)(128)(2,1)}, u32[]{:S(2)}) copy-start(bf16[96]{0:T(256)(128)(2,1)} %param.11) | copy-start | bytes 580
  3.9 4.2 copy-start.8
  265.1 5.5 %copy-start.6 = (bf16[16,2,96,640]{3,2,1,0:T(8,128)(2,1)S(1)}, bf16[16,2,96,640]{3,2,1,0:T(8,128)(2,1)}, u32[]{:S(2)}) copy-start(bf16[16,2,96,640]{3,2,1,0:T(8,128)(2,1)} %get-tuple-element.10) | copy-start | bytes 11796484
  275.6 2.1 copy-start.2
  277.8 3.3 copy-start.9
  284.3 1.8 copy-start.3
  286.7 1.0 copy-start.1
  379.7 1.4 copy-start
  402.4 77.6 %copy-start.5 = (bf16[16,64,192]{2,1,0:T(8,128)(2,1)S(1)}, bf16[16,64,192]{2,1,0:T(8,128)(2,1)}, u32[]{:S(2)}) copy-start(bf16[16,64,192]{2,1,0:T(8,128)(2,1)} %get-tuple-element.25) | copy-start | bytes 1179652
  478.0 3.5 copy-start.4

commit v2 on v1

--- a/solution.py
+++ b/solution.py
@@ -189,13 +189,158 @@
                 recv_add(h, ('2m',), 0, 0, 0, 2 * q)
 
 
+SLOTS = ((0, 0), (0, 1), (0, -1), (1, 0), (-1, 0), (1, 1), (1, -1), (-1, 1), (-1, -1),
+         (2, 0), (0, 2), (2, 1), (2, -1), (1, 2), (-1, 2), (2, 2))
+
+
+def slot_of(a, b):
+    return SLOTS.index(((a + 1) % 4 - 1, (b + 1) % 4 - 1))
+
+
+def swap_if(h, a, b):
+    return (b, a) if h == 0 else (a, b)
+
+
+HALVES = (0, 1)
+
+
+class Gather:
+    def __init__(self, pos, m, blk, width):
+        self.pos, self.m, self.blk, self.q = pos, m, blk, width // 4
+
+    def send(self, h, name, a, b, lo, n, ta, tb):
+        lo = 2 * self.q * h + lo
+        src = self.blk(slot_of(*swap_if(h, a, b)), lo, n)
+        dst = self.blk(slot_of(*swap_if(h, a - ta, b - tb)), lo, n)
+        self.m.start(('ag', h) + name, src, dst, self.pos.dev(*swap_if(h, ta, tb)))
+
+    def recv(self, h, *name):
+        self.m.recv(('ag', h) + name)
+
+    def second(self, h, a):
+        self.send(h, ('2p', a), a, 0, 0, 2 * self.q, 0, 1)
+        self.send(h, ('2m', a), a, 0, 0, 2 * self.q, 0, -1)
+
+    def second_forward(self, a):
+        for h in HALVES:
+            self.recv(h, '2p', a)
+            self.send(h, ('2pf', a), a, -1, 0, self.q, 0, 1)
+            self.recv(h, '2m', a)
+            self.send(h, ('2mf', a), a, 1, self.q, self.q, 0, -1)
+
+    def last(self, a):
+        for h in HALVES:
+            self.recv(h, '2pf', a)
+            self.recv(h, '2mf', a)
+
+    def begin(self):
+        q = self.q
+        for h in HALVES:
+            self.send(h, ('1p',), 0, 0, 0, 2 * q, 1, 0)
+            self.send(h, ('1m',), 0, 0, 0, 2 * q, -1, 0)
+        for h in HALVES:
+            self.second(h, 0)
+        for h in HALVES:
+            self.recv(h, '1p')
+            self.send(h, ('1pf',), -1, 0, 0, q, 1, 0)
+            self.second(h, -1)
+        for h in HALVES:
+            self.recv(h, '1m')
+            self.send(h, ('1mf',), 1, 0, q, q, -1, 0)
+            self.second(h, 1)
+        self.second_forward(0)
+
+    def middle(self):
+        for h in HALVES:
+            self.recv(h, '1pf')
+            self.recv(h, '1mf')
+            self.second(h, 2)
+
+    def run(self, hook=lambda first, n: None):
+        self.begin()
+        self.middle()
+        hook(0, 5)
+        self.second_forward(-1)
+        self.second_forward(1)
+        hook(5, 4)
+        self.second_forward(2)
+        self.last(0)
+        hook(9, 2)
+        self.last(-1)
+        self.last(1)
+        hook(11, 4)
+        self.last(2)
+        hook(15, 1)
+
+
+class Scatter:
+    def __init__(self, pos, m, part, recv_buf, rows, width):
+        self.pos, self.m, self.part, self.recv_buf = pos, m, part, recv_buf
+        self.rows, self.q = rows, width // 4
+        self.places = {}
+
+    def send(self, h, name, a, b, lo, n, ta, tb):
+        key = ('rs', h) + name
+        self.places[key] = sum(k for _, k in self.places.values()), n // self.q
+        first = self.places[key][0]
+        src = self.part.at[pl.ds(slot_of(*swap_if(1 - h, a, b)) * self.rows, self.rows), pl.ds(2 * self.q * h + lo, n)]
+        dst = self.recv_buf.at[:, pl.ds(first * self.q, n)]
+        self.m.start(key, src, dst, self.pos.dev(*swap_if(1 - h, ta, tb)))
+
+    def recv_add(self, h, name, a, b, lo, n):
+        key = ('rs', h) + name
+        self.m.recv(key)
+        there = pl.ds(self.places[key][0] * self.q, n)
+        here = pl.ds(2 * self.q * h + lo, n)
+        base = slot_of(*swap_if(1 - h, a, b)) * self.rows
+
+        @pl.loop(0, self.rows // 16)
+        def _(i):
+            mine = pl.ds(pl.multiple_of(base + i * 16, 16), 16)
+            theirs = pl.ds(pl.multiple_of(i * 16, 16), 16)
+            self.part[mine, here] = self.part[mine, here] + self.recv_buf[theirs, there]
+
+    def begin(self):
+        q = self.q
+        for b in (2, 1, -1, 0):
+            for h in HALVES:
+                self.send(h, ('1pf', b), 2, b, 0, q, 1, 0)
+                self.send(h, ('1mf', b), 2, b, q, q, -1, 0)
+
+    def finish(self):
+        q = self.q
+        order = (2, 1, -1, 0)
+        for b in order:
+            for h in HALVES:
+                self.recv_add(h, ('1pf', b), 1, b, 0, q)
+                self.send(h, ('1p', b), 1, b, 0, 2 * q, 1, 0)
+                self.recv_add(h, ('1mf', b), -1, b, q, q)
+                self.send(h, ('1m', b), -1, b, 0, 2 * q, -1, 0)
+        for b in order:
+            for h in HALVES:
+                self.recv_add(h, ('1p', b), 0, b, 0, 2 * q)
+                self.recv_add(h, ('1m', b), 0, b, 0, 2 * q)
+                if b == 2:
+                    self.send(h, ('2pf',), 0, 2, 0, q, 0, 1)
+                    self.send(h, ('2mf',), 0, 2, q, q, 0, -1)
+                if b == 1:
+                    self.recv_add(h, ('2pf',), 0, 1, 0, q)
+                    self.send(h, ('2p',), 0, 1, 0, 2 * q, 0, 1)
+                if b == -1:
+                    self.recv_add(h, ('2mf',), 0, -1, q, q)
+                    self.send(h, ('2m',), 0, -1, 0, 2 * q, 0, -1)
+                if b == 0:
+                    self.recv_add(h, ('2p',), 0, 0, 0, 2 * q)
+                    self.recv_add(h, ('2m',), 0, 0, 0, 2 * q)
+
+
 def torus_neighbours(pos):
     return [pos.dev(0, 1), pos.dev(0, -1), pos.dev(1, 0), pos.dev(-1, 0)]
 
 
 def offsets(side):
-    every = [(dy, dx) for dy in range(side) for dx in range(side) if (dy, dx) != (0, 0)]
-    return sorted(every, key=lambda o: min(o[0], side - o[0]) + min(o[1], side - o[1]))
+    return [(1, 1), (-1, -1), (1, -1), (-1, 1), (0, 1), (1, 0), (0, -1), (-1, 0),
+            (2, 2), (0, 2), (2, 0), (1, 2), (-1, 2), (2, 1), (2, -1)]
 
 
 def start_kernel(side, tok, wq, wgu, wo, table, tok_all, wq_all, wgu_all, wo_all, table_other,
@@ -289,31 +434,62 @@
     m2.drain()
 
 
-def gather_kernel(side, x, x_all, s2, r2, l_sem):
-    pos = Place(side)
-    me_chip = pos.chip(0, 0)
-    cp = pltpu.make_async_copy(x, x_all.at[me_chip], l_sem.at[0])
-    cp.start()
-    barrier(torus_neighbours(pos))
-    cp.wait()
-    m = Msgs(s2, r2)
-    torus_all_gather(pos, m, lambda p, lo, n: x_all.at[p, :, pl.ds(lo, n)], x_all.shape[2])
-    m.drain()
-
-
-def scatter_kernel(side, part_hbm, out, part, recv_buf, s1, r1, l_sem):
-    pos = Place(side)
-    barrier(torus_neighbours(pos))
-    width = out.shape[1]
-    loads = [pltpu.make_async_copy(part_hbm.at[i], part.at[i], l_sem.at[i]) for i in range(side * side)]
+def mlp_kernel(h_own, x_mid, wgu_hbm, wd_hbm, out, h_all, wgu, wd, act, part, recv_buf,
+               s1, r1, s2, r2, w_send, w_recv, l_sem):
+    pos = Place(4)
+    f32, bf16 = jnp.float32, jnp.bfloat16
+    rows, width = out.shape
+    ffb = act.shape[1]
+    half = ffb // 2
+    tile = 256
+    loads = [pltpu.make_async_copy(h_own, h_all.at[pl.ds(0, rows)], l_sem.at[0]),
+             pltpu.make_async_copy(wgu_hbm, wgu, l_sem.at[1]),
+             pltpu.make_async_copy(wd_hbm, wd.at[pos.c], l_sem.at[2])]
     for cp in loads:
         cp.start()
-    for cp in loads:
-        cp.wait()
+    barrier(torus_neighbours(pos) + [pos.partner])
+    push = pltpu.make_async_remote_copy(src_ref=wd_hbm, dst_ref=wd.at[pos.c], send_sem=w_send.at[0], recv_sem=w_recv.at[0],
+                                        device_id={AXIS: pos.partner}, device_id_type=MESH)
+    push.start()
+    loads[0].wait()
+    waited = []
+
+    def gate_up(first, n):
+        if not waited:
+            loads[1].wait()
+            waited.append(True)
+        mine = pl.ds(first * rows, n * rows)
+
+        @pl.loop(0, ffb // tile)
+        def _(i):
+            lo = pl.multiple_of(i * tile, tile)
+            h = h_all[mine, :]
+            g = jnp.dot(h, wgu[:, :, :, pl.ds(lo, tile)].reshape(width, tile), preferred_element_type=f32)
+            u = jnp.dot(h, wgu[:, :, :, pl.ds(pl.multiple_of(ffb + lo, tile), tile)].reshape(width, tile),
+                        preferred_element_type=f32)
+            act[mine, pl.ds(lo, tile)] = (jax.nn.silu(g) * u).astype(bf16)
+
+    def down(first, n):
+        mine = pl.ds(first * rows, n * rows)
+
+        @pl.loop(0, width // tile)
+        def _(i):
+            cols = pl.ds(pl.multiple_of(i * tile, tile), tile)
+            part[mine, cols] = jnp.dot(act[mine, :], wd[:, :, cols].reshape(2 * half, tile), preferred_element_type=f32)
+
     m = Msgs(s1, r1)
-    torus_reduce_scatter(pos, m, part, recv_buf, width)
-    out[...] = part[pos.chip(0, 0)]
+    Gather(pos, m, lambda s, lo, n: h_all.at[pl.ds(s * rows, rows), pl.ds(lo, n)], width).run(gate_up)
+    loads[2].wait()
+    push.wait()
+    m2 = Msgs(s2, r2)
+    scatter = Scatter(pos, m2, part, recv_buf, rows, width)
+    down(9, 7)
+    scatter.begin()
+    down(0, 9)
+    scatter.finish()
+    out[...] = (x_mid[...].astype(f32) + part[pl.ds(0, rows), :]).astype(bf16)
     m.drain()
+    m2.drain()
 
 
 def exchange_kernel(side, src, dst, sems, recvs, l_sem):
@@ -411,7 +587,6 @@
         gains = wq_all[..., width:width + 2].reshape(d_model, 2)
         gain_attn, gain_mlp = gains[:, 0], gains[:, 1]
         wq_own = wq_all.reshape(d_model, pad_width)
-        wgu_own = wgu_all.reshape(d_model, 2 * ffb)
         wo_full = wo_all.reshape(q_width, d_model)
 
         ids = tok_all.reshape(chips * seq)
@@ -469,40 +644,20 @@
         x_mid = (x_own.astype(f32) + attn_proj).astype(bf16)
         normed_mlp = rms_norm(x_mid, gain_mlp)
 
-        h_all = pl.pallas_call(
-            functools.partial(gather_kernel, side), name='gather_hidden',
-            out_shape=jax.ShapeDtypeStruct((chips, seq, d_model), bf16),
-            in_specs=[pl.BlockSpec(memory_space=pltpu.VMEM)], out_specs=pl.BlockSpec(memory_space=pl.ANY),
-            scratch_shapes=[dma(AG_MSGS), dma(AG_MSGS), dma(1)],
+        vmem = pl.BlockSpec(memory_space=pltpu.VMEM)
+        layer_out = pl.pallas_call(
+            mlp_kernel, name='mlp',
+            out_shape=jax.ShapeDtypeStruct((seq, d_model), bf16),
+            in_specs=[ANY, vmem, ANY, ANY], out_specs=vmem,
+            scratch_shapes=[pltpu.VMEM((chips * seq, d_model), bf16),
+                            pltpu.VMEM((chips, 2, rows, 2 * ffb), bf16),
+                            pltpu.VMEM((2, ffb // 2, d_model), bf16),
+                            pltpu.VMEM((chips * seq, ffb), bf16),
+                            pltpu.VMEM((chips * seq, d_model), f32),
+                            pltpu.VMEM((seq, d_model * n_off), f32),
+                            dma(AG_MSGS), dma(AG_MSGS), dma(RS_MSGS), dma(RS_MSGS), dma(1), dma(1), dma(3)],
             compiler_params=params(4),
-        )(normed_mlp)
-
-        wd_other = pl.pallas_call(
-            swap_kernel, name='swap_down',
-            out_shape=jax.ShapeDtypeStruct(w_down.shape, bf16),
-            in_specs=[ANY], out_specs=ANY, scratch_shapes=[dma(1), dma(1)],
-            compiler_params=params(6),
-        )(w_down)
-        first = lax.rem(me, 2) == 0
-
-        gate_up = jnp.dot(h_all.reshape(chips * seq, d_model), wgu_own, preferred_element_type=f32)
-        act = (jax.nn.silu(gate_up[:, :ffb]) * gate_up[:, ffb:]).astype(bf16)
-        half = ffb // 2
-        act_own = lax.dynamic_slice_in_dim(act, lax.rem(me, 2) * half, half, axis=1)
-        act_other = lax.dynamic_slice_in_dim(act, (1 - lax.rem(me, 2)) * half, half, axis=1)
-        down = (jnp.dot(act_own, w_down, preferred_element_type=f32)
-                + jnp.dot(act_other, wd_other, preferred_element_type=f32))
-
-        total = pl.pallas_call(
-            functools.partial(scatter_kernel, side), name='scatter_down',
-            out_shape=jax.ShapeDtypeStruct((seq, d_model), f32),
-            in_specs=[ANY], out_specs=pl.BlockSpec(memory_space=pltpu.VMEM),
-            scratch_shapes=[pltpu.VMEM((chips, seq, d_model), f32),
-                            pltpu.VMEM((seq, d_model * n_off), f32),
-                            dma(RS_MSGS), dma(RS_MSGS), dma(chips)],
-            compiler_params=params(5),
-        )(down.reshape(chips, seq, d_model))
-        layer_out = (x_mid.astype(f32) + total).astype(bf16)
+        )(normed_mlp, x_mid, wgu_all, w_down)
         return layer_out[None], key_own, val_own
 
     return jax.shard_map(
@@ -512,13 +667,3 @@
         out_specs=(P(batch_axes, None, None), P(batch_axes, None, None, None), P(batch_axes, None, None, None)),
         check_vma=False,
     )
-
-
-def swap_kernel(src, dst, send_sem, recv_sem):
-    me = lax.axis_index(AXIS)
-    partner = me + 1 - 2 * lax.rem(me, 2)
-    barrier([partner])
-    cp = pltpu.make_async_remote_copy(src_ref=src, dst_ref=dst, send_sem=send_sem.at[0], recv_sem=recv_sem.at[0],
-                                      device_id={AXIS: partner}, device_id_type=MESH)
-    cp.start()
-    cp.wait()

time: 486 us -> 442 us (0.909)
  matrix products: 71.6 us -> 43.1 us
  Pallas kernels: 354 us -> 344 us
    dot_general x3 -> x0, matrix products: 28.5 us -> none  [the longest x1 11.6 us: device_step(): jnp.dot(act_other, wd_other, preferred_element_type=f32)]
    pallas_call x3 -> x1, Pallas kernels: 114 us -> 110 us  [device_step(): pl.pallas_call(mlp_kernel, name='mlp', out_shape=jax.ShapeDtypeStruct((se...]
where the time goes in v2:
time: 442 us; the launch traced here: 439 us
  Pallas kernels  344 us (78%)
  matrix products  43.1 us (10%)
  local copies, waits for them, and re-layouts  34.1 us (8%)
  other arithmetic  16.3 us (4%)
    pallas_call x1, Pallas kernels, device_step(): pl.pallas_call(functools.partial(start_kernel, side), name='start', out_s...  134 us
    pallas_call x1, Pallas kernels, device_step(): pl.pallas_call(mlp_kernel, name='mlp', out_shape=jax.ShapeDtypeStruct((se...  110 us
    pallas_call x1, Pallas kernels, device_step(): pl.pallas_call(functools.partial(embed_kernel, side), name='embed', out_s...  80.2 us
    dot_general x2, matrix products, pick(): return jnp.dot(hot, table, preferred_element_type=f32)  26 us
    pallas_call x1, Pallas kernels, device_step(): pl.pallas_call(functools.partial(exchange_kernel, side), name='to_sequenc...  20.2 us
    dot_general x1, matrix products, device_step(): attn_proj = jnp.dot(ctx_own, wo_full, preferred_element_type=f32)  9.89 us

profile of v2, /device:TPU:96, one launch (start us, length us, event | category | flops | bytes accessed | tf_op | source)
XLA Modules:
  0.0 438.8 jit_solution(8764886271538231803)
XLA Ops:
  0.7 2.4 fusion.26
  5.3 2.1 reshape.192
  8.0 3.2 concatenate.15.wq
  11.2 133.7 %start.1 = (s32[16,1,64]{2,1,0:T(1,128)}, bf16[16,2,96,640]{3,2,1,0:T(8,128)(2,1)}, bf16[16,2,96,1024]{3,2,1,0:T(8,128)(2,1)}, bf16[16,2,96,3072]{3,2,1,0:T(8,128)(2,1)}, bf16[1002,3072]{1,0:T(8,128)(2,1)}) custom-call(s32[1,64]{1,0:T(1,128)} %tok.1, bf16[16,96,640]{2,1,0:T(8,128)(2,1)} %concatenate.15.wq, bf16[96,16384]{1,0:T(8,128)(2,1)} %wgu.1, ...), custom_call_target="tpu_custom_call" | custom-call | tf_op jit(solution)/shard_map/start/pallas_call | solution.py:574
  145.8 12.5 %fusion.3 = f32[1024,3072]{1,0:T(8,128)} fusion(bf16[1002,3072]{1,0:T(8,128)(2,1)} %table.1, s32[1024]{0:T(1024)S(1)} %sub.45), kind=kOutput, calls=%fused_computation.8 | convolution fusion | flops 6305064960 | bytes 18743296 | tf_op jit(solution)/shard_map/dot_general | solution.py:597
  158.4 13.5 %add_convert_fusion = bf16[1024,3072]{1,0:T(8,128)(2,1)} fusion(f32[1024,3072]{1,0:T(8,128)} %fusion.3, bf16[1002,3072]{1,0:T(8,128)(2,1)} %get-tuple-element.9, s32[1024]{0:T(1024)S(1)} %sub.49), kind=kOutput, calls=%fused_computation.5 | convolution fusion | flops 6311356416 | bytes 25034752 | tf_op jit(solution)/shard_map/dot_general | solution.py:597
  171.9 80.2 %embed.1 = bf16[16,64,3072]{2,1,0:T(8,128)(2,1)} custom-call(bf16[16,64,3072]{2,1,0:T(8,128)(2,1)} %bitcast.48), custom_call_target="tpu_custom_call" | custom-call | tf_op jit(solution)/shard_map/embed/pallas_call | solution.py:602
  252.1 4.1 fusion
  256.2 1.4 slice.55
  258.4 5.5 %fusion.2 = bf16[16,64,3072]{2,1,0:T(8,128)(2,1)S(1)} fusion(bf16[16,64,3072]{2,1,0:T(8,128)(2,1)} %embed.1, f32[3072]{0:T(1024)S(1)} %bitcast.59, f32[16,64]{1,0:T(8,128)S(1)} %add_rsqrt_fusion), kind=kLoop, calls=%fused_computation.4 | loop fusion | flops 12582912 | bytes 12599296 | tf_op jit(solution)/shard_map/convert_element_type | solution.py:525
  263.9 5.0 %fusion.4 = f32[1024,576]{1,0:T(8,128)S(1)} fusion(bf16[1024,3072]{1,0:T(8,128)(2,1)S(1)} %bitcast.49, bf16[3072,640]{1,0:T(8,128)(2,1)S(1)} %bitcast.58), kind=kOutput, calls=%fused_computation.9 | convolution fusion | flops 3623878656 | bytes 12582912 | tf_op jit(solution)/shard_map/slice | solution.py:615
  269.0 2.0 fusion.25
  271.1 1.9 reshape.201
  273.0 1.6 fusion.28
  275.9 1.9 reshape.200
  277.8 1.2 fusion.29
  281.4 1.3 slice.86
  283.0 1.6 fusion.11
  287.1 2.7 pad_maximum_fusion.src
  289.8 20.2 %to_sequences.1 = bf16[16,64,576]{2,1,0:T(8,128)(2,1)} custom-call(bf16[16,64,576]{2,1,0:T(8,128)(2,1)} %pad_maximum_fusion.src), custom_call_target="tpu_custom_call" | custom-call | tf_op jit(solution)/shard_map/to_sequences/pallas_call | solution.py:630
  310.1 1.7 fusion.27
  312.7 9.9 %fusion.13 = (f32[64]{0:T(128)S(1)}, bf16[64,3072]{1,0:T(8,128)(2,1)S(1)}) fusion(bf16[64,3072]{1,0:T(8,128)(2,1)S(1)} %reshape.204, bf16[3072,3072]{1,0:T(8,128)(2,1)} %bitcast.46, bf16[16,64,3072]{2,1,0:T(8,128)(2,1)} %embed.1, s32[]{:T(128)S(6)} %select_n.8), kind=kOutput, calls=%fused_computation.32 | convolution fusion | flops 1209139200 | bytes 20054276 | tf_op jit(solution)/shard_map/dot_general | solution.py:643
  324.1 109.8 %mlp.1 = bf16[64,3072]{1,0:T(8,128)(2,1)} custom-call(bf16[64,3072]{1,0:T(8,128)(2,1)} %fusion.15.h_own, bf16[64,3072]{1,0:T(8,128)(2,1)} %copy-done.1, bf16[16,2,96,1024]{3,2,1,0:T(8,128)(2,1)} %get-tuple-element.12.wgu_hbm, bf16[256,3072]{1,0:T(8,128)(2,1)} %wd_hbm.1), custom_call_target="tpu_custom_call" | custom-call | tf_op jit(solution)/shard_map/mlp/pallas_call | solution.py:648
  436.8 1.8 copy.64
  (51 shorter events, 16.3 us)
Async XLA Ops:
  0.6 7.0 %copy-start.5 = (bf16[96]{0:T(256)(128)(2,1)S(1)}, bf16[96]{0:T(256)(128)(2,1)}, u32[]{:S(2)}) copy-start(bf16[96]{0:T(256)(128)(2,1)} %param.11) | copy-start | bytes 580
  0.6 7.2 %copy-start.6 = (bf16[96]{0:T(256)(128)(2,1)S(1)}, bf16[96]{0:T(256)(128)(2,1)}, u32[]{:S(2)}) copy-start(bf16[96]{0:T(256)(128)(2,1)} %param.14) | copy-start | bytes 580
  258.4 5.5 %copy-start.4 = (bf16[16,2,96,640]{3,2,1,0:T(8,128)(2,1)S(1)}, bf16[16,2,96,640]{3,2,1,0:T(8,128)(2,1)}, u32[]{:S(2)}) copy-start(bf16[16,2,96,640]{3,2,1,0:T(8,128)(2,1)} %get-tuple-element.10) | copy-start | bytes 11796484
  268.9 2.1 copy-start.2
  269.0 5.6 %copy-start.7 = (f32[48]{0:T(128)S(1)}, f32[48]{0:T(128)}, u32[]{:S(2)}) copy-start(f32[48]{0:T(128)} %param.17) | copy-start | bytes 580
  277.8 1.8 copy-start.3
  280.2 1.0 copy-start
  322.6 1.6 copy-start.1

commit v3 on v2

v3 whole, which is shorter than its diff:
```python
import jax
import jax.numpy as jnp
from jax import lax
from jax.experimental import pallas as pl
from jax.experimental.pallas import tpu as pltpu
from jax.sharding import PartitionSpec as P

NORM_EPS = 1e-5
ROPE_THETA = 10000.0
AXIS = 'fsdp'
MESH = pl.DeviceIdType.MESH
ANY = pl.BlockSpec(memory_space=pl.ANY)
VMEM_LIMIT = 60 * 1024 * 1024


class Place:
    def __init__(self, side):
        me = lax.axis_index(AXIS)
        self.side = side
        self.c = lax.rem(me, 2)
        chip = lax.div(me, 2)
        self.y = lax.div(chip, side)
        self.x = lax.rem(chip, side)
        self.me = me
        self.partner = me + 1 - 2 * self.c

    def chip(self, dy, dx):
        s = self.side
        return lax.rem(self.y + dy + s, s) * s + lax.rem(self.x + dx + s, s)

    def dev(self, dy, dx):
        return self.chip(dy, dx) * 2 + self.c


def barrier(devices):
    sem = pltpu.get_barrier_semaphore()
    for d in devices:
        pl.semaphore_signal(sem, inc=1, device_id={AXIS: d}, device_id_type=MESH)
    pl.semaphore_wait(sem, len(devices))


class Msgs:
    def __init__(self, send_sem, recv_sem):
        self.send_sem, self.recv_sem = send_sem, recv_sem
        self.index, self.copies = {}, []

    def start(self, name, src, dst, dev):
        i = len(self.copies)
        self.index[name] = i
        copy = pltpu.make_async_remote_copy(
            src_ref=src, dst_ref=dst, send_sem=self.send_sem.at[i], recv_sem=self.recv_sem.at[i],
            device_id={AXIS: dev}, device_id_type=MESH)
        copy.start()
        self.copies.append(copy)

    def recv(self, name):
        self.copies[self.index[name]].wait_recv()

    def drain(self):
        for copy in self.copies:
            copy.wait_send()


AG_MSGS = 40
RS_MSGS = 40


SLOTS = ((0, 0), (0, 1), (0, -1), (1, 0), (-1, 0), (1, 1), (1, -1), (-1, 1), (-1, -1),
         (2, 0), (0, 2), (2, 1), (2, -1), (1, 2), (-1, 2), (2, 2))


def slot_of(a, b):
    return SLOTS.index(((a + 1) % 4 - 1, (b + 1) % 4 - 1))


def swap_if(h, a, b):
    return (b, a) if h == 0 else (a, b)


HALVES = (0, 1)


class Gather:
    def __init__(self, pos, m, blk, width, by_chip=False):
        self.pos, self.m, self.blk, self.q, self.by_chip = pos, m, blk, width // 4, by_chip

    def send(self, h, name, a, b, lo, n, ta, tb):
        lo = 2 * self.q * h + lo
        if self.by_chip:
            src = dst = self.blk(self.pos.chip(*swap_if(h, a, b)), lo, n)
        else:
            src = self.blk(slot_of(*swap_if(h, a, b)), lo, n)
            dst = self.blk(slot_of(*swap_if(h, a - ta, b - tb)), lo, n)
        self.m.start(('ag', h) + name, src, dst, self.pos.dev(*swap_if(h, ta, tb)))

    def recv(self, h, *name):
        self.m.recv(('ag', h) + name)

    def second(self, h, a):
        self.send(h, ('2p', a), a, 0, 0, 2 * self.q, 0, 1)
        self.send(h, ('2m', a), a, 0, 0, 2 * self.q, 0, -1)

    def second_forward(self, a):
        for h in HALVES:
            self.recv(h, '2p', a)
            self.send(h, ('2pf', a), a, -1, 0, self.q, 0, 1)
            self.recv(h, '2m', a)
            self.send(h, ('2mf', a), a, 1, self.q, self.q, 0, -1)

    def last(self, a):
        for h in HALVES:
            self.recv(h, '2pf', a)
            self.recv(h, '2mf', a)

    def begin(self):
        q = self.q
        for h in HALVES:
            self.send(h, ('1p',), 0, 0, 0, 2 * q, 1, 0)
            self.send(h, ('1m',), 0, 0, 0, 2 * q, -1, 0)
        for h in HALVES:
            self.second(h, 0)
        for h in HALVES:
            self.recv(h, '1p')
            self.send(h, ('1pf',), -1, 0, 0, q, 1, 0)
            self.second(h, -1)
        for h in HALVES:
            self.recv(h, '1m')
            self.send(h, ('1mf',), 1, 0, q, q, -1, 0)
            self.second(h, 1)
        self.second_forward(0)

    def middle(self):
        for h in HALVES:
            self.recv(h, '1pf')
            self.recv(h, '1mf')
            self.second(h, 2)

    def run(self, hook=lambda first, n: None):
        self.begin()
        self.rest(hook)

    def rest(self, hook, before_last=lambda: None):
        self.middle()
        hook(0, 5)
        self.second_forward(-1)
        self.second_forward(1)
        hook(5, 4)
        self.second_forward(2)
        before_last()
        self.last(0)
        hook(9, 2)
        self.last(-1)
        self.last(1)
        hook(11, 4)
        self.last(2)
        hook(15, 1)


class Scatter:
    def __init__(self, pos, m, part, recv_buf, rows, width):
        self.pos, self.m, self.part, self.recv_buf = pos, m, part, recv_buf
        self.rows, self.q = rows, width // 4
        self.places = {}

    def send(self, h, name, a, b, lo, n, ta, tb):
        key = ('rs', h) + name
        self.places[key] = sum(k for _, k in self.places.values()), n // self.q
        first = self.places[key][0]
        src = self.part.at[pl.ds(slot_of(*swap_if(1 - h, a, b)) * self.rows, self.rows), pl.ds(2 * self.q * h + lo, n)]
        dst = self.recv_buf.at[:, pl.ds(first * self.q, n)]
        self.m.start(key, src, dst, self.pos.dev(*swap_if(1 - h, ta, tb)))

    def recv_add(self, h, name, a, b, lo, n):
        key = ('rs', h) + name
        self.m.recv(key)
        there = pl.ds(self.places[key][0] * self.q, n)
        here = pl.ds(2 * self.q * h + lo, n)
        base = slot_of(*swap_if(1 - h, a, b)) * self.rows

        @pl.loop(0, self.rows // 16)
        def _(i):
            mine = pl.ds(pl.multiple_of(base + i * 16, 16), 16)
            theirs = pl.ds(pl.multiple_of(i * 16, 16), 16)
            self.part[mine, here] = self.part[mine, here] + self.recv_buf[theirs, there]

    def begin(self):
        q = self.q
        for b in (2, 1, -1, 0):
            for h in HALVES:
                self.send(h, ('1pf', b), 2, b, 0, q, 1, 0)
                self.send(h, ('1mf', b), 2, b, q, q, -1, 0)

    def finish(self, hook=lambda i: None):
        q = self.q
        order = (2, 1, -1, 0)
        calls = iter(range(16))
        for b in order:
            for h in HALVES:
                self.recv_add(h, ('1pf', b), 1, b, 0, q)
                self.send(h, ('1p', b), 1, b, 0, 2 * q, 1, 0)
                self.recv_add(h, ('1mf', b), -1, b, q, q)
                self.send(h, ('1m', b), -1, b, 0, 2 * q, -1, 0)
                hook(next(calls))
        for b in order:
            for h in HALVES:
                self.recv_add(h, ('1p', b), 0, b, 0, 2 * q)
                self.recv_add(h, ('1m', b), 0, b, 0, 2 * q)
                if b == 2:
                    self.send(h, ('2pf',), 0, 2, 0, q, 0, 1)
                    self.send(h, ('2mf',), 0, 2, q, q, 0, -1)
                if b == 1:
                    self.recv_add(h, ('2pf',), 0, 1, 0, q)
                    self.send(h, ('2p',), 0, 1, 0, 2 * q, 0, 1)
                if b == -1:
                    self.recv_add(h, ('2mf',), 0, -1, q, q)
                    self.send(h, ('2m',), 0, -1, 0, 2 * q, 0, -1)
                if b == 0:
                    self.recv_add(h, ('2p',), 0, 0, 0, 2 * q)
                    self.recv_add(h, ('2m',), 0, 0, 0, 2 * q)
                hook(next(calls))


def torus_neighbours(pos):
    return [pos.dev(0, 1), pos.dev(0, -1), pos.dev(1, 0), pos.dev(-1, 0)]


def offsets(side):
    return [(1, 1), (-1, -1), (1, -1), (-1, 1), (0, 1), (1, 0), (0, -1), (-1, 0),
            (2, 2), (0, 2), (2, 0), (1, 2), (-1, 2), (2, 1), (2, -1)]


def remote(src, dst, sems, i, dev):
    return pltpu.make_async_remote_copy(src_ref=src, dst_ref=dst, send_sem=sems.at[0, i], recv_sem=sems.at[1, i],
                                        device_id={AXIS: dev}, device_id_type=MESH)


def front_kernel(tok, gains, wqkv, cos2, sin2, wgu, wo, table,
                 x_own, mine, wgu_all, wo_all, gain_rows,
                 tok_all, tok_col, tbl, hot, part, recv_buf, x_all, wq_out, wq, normed, proj, packed,
                 t_sem, q_sem, qf_sem, g_sem, gf_sem, o_sem, of_sem, r_sem, a_sem, e_sem, l_sem):
    f32, bf16 = jnp.float32, jnp.bfloat16
    pos = Place(4)
    offs = offsets(4)
    here = pos.chip(0, 0)
    rows, lanes = wq_out.shape[1], 128
    seq, width = x_own.shape
    n_slots = len(SLOTS)
    n_off = len(offs)
    ff = wgu.shape[1] // 2
    ffb = ff // n_slots
    head_dim = wqkv.shape[1] // (6 * n_slots)
    table_rows = table.shape[0]
    tile = 256
    loads = [pltpu.make_async_copy(table, tbl.at[pos.c], l_sem.at[0]),
             pltpu.make_async_copy(tok, tok_all.at[0], l_sem.at[1]),
             pltpu.make_async_copy(wo, wo_all.at[here, pos.c], l_sem.at[2])]
    for j in (0, 1):
        src = wgu.at[:, pl.ds(pl.multiple_of(j * ff + here * ffb, 128), ffb)]
        loads.append(pltpu.make_async_copy(src, wgu_all.at[here, pos.c, :, pl.ds(j * ffb, ffb)], l_sem.at[3 + j]))
    for cp in loads:
        cp.start()
    barrier([pos.dev(dy, dx) for dy, dx in offs] + [pos.partner])

    toks = [remote(tok, tok_all.at[slot_of(-dy, -dx)], t_sem, i, pos.dev(dy, dx)) for i, (dy, dx) in enumerate(offs)]
    for cp in toks:
        cp.start()
    swap = remote(table, tbl.at[pos.c], t_sem, n_off, pos.partner)
    swap.start()

    for p in range(n_slots):
        for k in range(6):
            j, hd = k // 2, k % 2
            lo = (j * 2 * n_slots + p * 2 + hd) * head_dim
            block = jnp.concatenate([wqkv[:, lo:lo + head_dim], jnp.zeros((rows, lanes - head_dim), bf16)], axis=1)
            if k == 4:
                block = block + gains[...]
            wq_out[p, :, k * lanes:(k + 1) * lanes] = block
    my_rows = pl.ds(pl.multiple_of(pos.me * rows, 32), rows)
    qs = [remote(wq_out.at[pos.chip(dy, dx)], wq.at[my_rows], q_sem, i, pos.dev(dy, dx)) for i, (dy, dx) in enumerate(offs)]
    for cp in qs:
        cp.start()
    wq[my_rows, :] = wq_out[here]

    loads[1].wait()
    for i, (dy, dx) in enumerate(offs):
        toks[i].wait_recv()
    for s in range(n_slots):
        column = jnp.transpose(tok_all[s].astype(f32))
        tok_col[pl.ds(s * seq, seq), :] = column[:seq, 0:1]
    loads[0].wait()
    swap.wait_recv()
    group = hot.shape[1]
    for g in range(n_slots * seq // group):
        mine_rows = pl.ds(g * group, group)
        for cc in (0, 1):
            ids = lax.broadcasted_iota(jnp.int32, (group, table_rows), 1) + (here * 2 + cc) * table_rows
            hot[cc] = jnp.where(tok_col[mine_rows, :] == ids.astype(f32), 1.0, 0.0).astype(bf16)

        @pl.loop(0, width // tile)
        def _(i):
            cols = pl.ds(pl.multiple_of(i * tile, tile), tile)
            total = (jnp.dot(hot[0], tbl[0, :, cols], preferred_element_type=f32)
                     + jnp.dot(hot[1], tbl[1, :, cols], preferred_element_type=f32))
            part[mine_rows, cols] = total.astype(bf16)

    m = Msgs(r_sem.at[0], r_sem.at[1])
    scatter = Scatter(pos, m, part, recv_buf, seq, width)
    scatter.begin()

    fwd = []

    def forward(sems, i, ref):
        cp = remote(ref, ref, sems, i, pos.partner)
        cp.start()
        fwd.append(cp)
        return cp

    q_fwd = [forward(qf_sem, n_off, wq.at[my_rows])]
    for i, (dy, dx) in enumerate(offs):
        qs[i].wait_recv()
        q_fwd.append(forward(qf_sem, i, wq.at[pl.ds(pl.multiple_of(pos.dev(-dy, -dx) * rows, 32), rows)]))
    for cp in q_fwd:
        cp.wait_recv()
    for k in range(width // lanes):
        square = jnp.transpose(wq[pl.ds(k * lanes, lanes), 4 * lanes:5 * lanes].astype(f32))
        gain_rows[:, k * lanes:(k + 1) * lanes] = square[head_dim:head_dim + 8, :]

    gs = []
    for i, (dy, dx) in enumerate(offs):
        for j in (0, 1):
            src = wgu.at[:, pl.ds(pl.multiple_of(j * ff + pos.chip(dy, dx) * ffb, 128), ffb)]
            gs.append(remote(src, wgu_all.at[here, pos.c, :, pl.ds(j * ffb, ffb)], g_sem, 2 * i + j, pos.dev(dy, dx)))

    def send_gate_up(i):
        for cp in gs[2 * i:2 * i + 2]:
            cp.start()

    scatter.finish(send_gate_up)
    x_all[pl.ds(0, seq), :] = part[pl.ds(0, seq), :]
    x_own[...] = part[pl.ds(0, seq), :]

    sends = []

    def attend(first, n):
        base = first * seq

        @pl.loop(0, n * seq // 16)
        def _(i):
            x = x_all[pl.ds(pl.multiple_of(base + i * 16, 16), 16), :].astype(f32)
            inv = lax.rsqrt(jnp.mean(x * x, axis=-1, keepdims=True) + NORM_EPS)
            normed[pl.ds(pl.multiple_of(i * 16, 16), 16), :] = (x * inv * gain_rows[0:1, :]).astype(bf16)

        @pl.loop(0, 3)
        def _(i):
            cols = pl.ds(pl.multiple_of(i * tile, tile), tile)
            proj[pl.ds(0, n * seq), cols] = jnp.dot(normed[pl.ds(0, n * seq), :], wq[:, cols], preferred_element_type=f32)

        lane = lax.broadcasted_iota(jnp.int32, (seq, lanes), 1)
        causal = lax.broadcasted_iota(jnp.int32, (seq, seq), 0) >= lax.broadcasted_iota(jnp.int32, (seq, seq), 1)

        def rope(u):
            other = jnp.where(lane < head_dim // 2, pltpu.roll(u, lanes - head_dim // 2, 1), pltpu.roll(u, head_dim // 2, 1))
            return (u * cos2[...] + other * sin2[...]).astype(bf16)

        @pl.loop(0, n)
        def _(s):
            mine_rows = pl.ds(pl.multiple_of(s * seq, seq), seq)
            for hd in (0, 1):
                q = rope(proj[mine_rows, hd * lanes:(hd + 1) * lanes])
                k = rope(proj[mine_rows, (2 + hd) * lanes:(3 + hd) * lanes])
                v = proj[mine_rows, (4 + hd) * lanes:(5 + hd) * lanes].astype(bf16)
                scores = lax.dot_general(q, k, (((1,), (1,)), ((), ())), preferred_element_type=f32) * (head_dim ** -0.5)
                scores = jnp.where(causal, scores, -jnp.inf)
                e = jnp.exp(scores - jnp.max(scores, axis=-1, keepdims=True))
                probs = (e / jnp.sum(e, axis=-1, keepdims=True)).astype(bf16)
                context = jnp.dot(probs, v, preferred_element_type=f32).astype(bf16)
                packed[first + s, :, hd * lanes:(hd + 1) * lanes] = context
                packed[first + s, :, (2 + hd) * lanes:(3 + hd) * lanes] = k
                packed[first + s, :, (4 + hd) * lanes:(5 + hd) * lanes] = v

        for s in range(first, first + n):
            if s == 0:
                cp = pltpu.make_async_copy(packed.at[0], mine.at[here], l_sem.at[5])
            else:
                cp = remote(packed.at[s], mine.at[here], e_sem, s - 1, pos.dev(*SLOTS[s]))
            cp.start()
            sends.append(cp)

    m2 = Msgs(a_sem.at[0], a_sem.at[1])
    gather = Gather(pos, m2, lambda s, lo, n: x_all.at[pl.ds(s * seq, seq), pl.ds(lo, n)], width)
    m3 = Msgs(o_sem.at[0], o_sem.at[1])
    out_gather = Gather(pos, m3, lambda p, lo, n: wo_all.at[p, pos.c, :, pl.ds(lo, n)], width, by_chip=True)
    for cp in loads[2:]:
        cp.wait()
    forward(gf_sem, n_off, wgu_all.at[here, pos.c])
    gather.begin()
    gather.rest(attend, out_gather.begin)

    def forward_out(first, n):
        for s in range(first, first + n):
            forward(of_sem, s, wo_all.at[pos.chip(*SLOTS[s]), pos.c])

    for i, (dy, dx) in enumerate(offs):
        gs[2 * i].wait_recv()
        gs[2 * i + 1].wait_recv()
        forward(gf_sem, i, wgu_all.at[pos.chip(-dy, -dx), pos.c])
    out_gather.rest(forward_out)
    for cp in sends:
        cp.wait()
    for cp in toks + qs + gs + [swap]:
        cp.wait_send()
    for cp in fwd[:1 + n_off]:
        cp.wait_send()
    for cp in fwd[1 + n_off:]:
        cp.wait()
    for msgs in (m, m2, m3):
        msgs.drain()


def mlp_kernel(h_own, x_mid, wgu_hbm, wd_hbm, out, h_all, wgu, wd, act, part, recv_buf,
               s1, r1, s2, r2, w_send, w_recv, l_sem):
    pos = Place(4)
    f32, bf16 = jnp.float32, jnp.bfloat16
    rows, width = out.shape
    ffb = act.shape[1]
    half = ffb // 2
    tile = 256
    loads = [pltpu.make_async_copy(h_own, h_all.at[pl.ds(0, rows)], l_sem.at[0]),
             pltpu.make_async_copy(wgu_hbm, wgu, l_sem.at[1]),
             pltpu.make_async_copy(wd_hbm, wd.at[pos.c], l_sem.at[2])]
    for cp in loads:
        cp.start()
    barrier(torus_neighbours(pos) + [pos.partner])
    push = pltpu.make_async_remote_copy(src_ref=wd_hbm, dst_ref=wd.at[pos.c], send_sem=w_send.at[0], recv_sem=w_recv.at[0],
                                        device_id={AXIS: pos.partner}, device_id_type=MESH)
    push.start()
    loads[0].wait()
    waited = []

    def gate_up(first, n):
        if not waited:
            loads[1].wait()
            waited.append(True)
        mine = pl.ds(first * rows, n * rows)

        @pl.loop(0, ffb // tile)
        def _(i):
            lo = pl.multiple_of(i * tile, tile)
            h = h_all[mine, :]
            g = jnp.dot(h, wgu[:, :, :, pl.ds(lo, tile)].reshape(width, tile), preferred_element_type=f32)
            u = jnp.dot(h, wgu[:, :, :, pl.ds(pl.multiple_of(ffb + lo, tile), tile)].reshape(width, tile),
                        preferred_element_type=f32)
            act[mine, pl.ds(lo, tile)] = (jax.nn.silu(g) * u).astype(bf16)

    def down(first, n):
        mine = pl.ds(first * rows, n * rows)

        @pl.loop(0, width // tile)
        def _(i):
            cols = pl.ds(pl.multiple_of(i * tile, tile), tile)
            part[mine, cols] = jnp.dot(act[mine, :], wd[:, :, cols].reshape(2 * half, tile), preferred_element_type=f32)

    m = Msgs(s1, r1)
    Gather(pos, m, lambda s, lo, n: h_all.at[pl.ds(s * rows, rows), pl.ds(lo, n)], width).run(gate_up)
    loads[2].wait()
    push.wait()
    m2 = Msgs(s2, r2)
    scatter = Scatter(pos, m2, part, recv_buf, rows, width)
    down(9, 7)
    scatter.begin()
    down(0, 9)
    scatter.finish()
    out[...] = (x_mid[...].astype(f32) + part[pl.ds(0, rows), :]).astype(bf16)
    m.drain()
    m2.drain()


def exchange_kernel(side, src, dst, sems, recvs, l_sem):
    pos = Place(side)
    offs = offsets(side)
    me_chip = pos.chip(0, 0)
    barrier([pos.dev(dy, dx) for dy, dx in offs])
    copies = []
    for i, (dy, dx) in enumerate(offs):
        cp = pltpu.make_async_remote_copy(
            src_ref=src.at[pos.chip(dy, dx)], dst_ref=dst.at[me_chip], send_sem=sems.at[i], recv_sem=recvs.at[i],
            device_id={AXIS: pos.dev(dy, dx)}, device_id_type=MESH)
        cp.start()
        copies.append(cp)
    own = pltpu.make_async_copy(src.at[me_chip], dst.at[me_chip], l_sem.at[0])
    own.start()
    own.wait()
    for cp in copies:
        cp.wait()


def dma(n):
    return pltpu.SemaphoreType.DMA((n,))


def dma2(n):
    return pltpu.SemaphoreType.DMA((2, n))


def params(cid):
    return pltpu.CompilerParams(collective_id=cid, has_side_effects=True, vmem_limit_bytes=VMEM_LIMIT)


def rms_norm(hidden, gain):
    h_f32 = hidden.astype(jnp.float32)
    inv_rms = lax.rsqrt(jnp.mean(h_f32 * h_f32, axis=-1, keepdims=True) + NORM_EPS)
    return (h_f32 * inv_rms * gain.astype(jnp.float32)).astype(jnp.bfloat16)


def rope_tables(rope_scale, seq_len, lanes):
    half_dim = rope_scale.shape[0]
    freq_expo = jnp.arange(half_dim, dtype=jnp.float32) * (2.0 / (2 * half_dim))
    inv_freq = 1.0 / (rope_scale * jnp.power(ROPE_THETA, freq_expo))
    angles = jnp.arange(seq_len, dtype=jnp.float32)[:, None] * inv_freq[None, :]
    cos, sin = jnp.cos(angles), jnp.sin(angles)
    rest = jnp.zeros((seq_len, lanes - 2 * half_dim), jnp.float32)
    return jnp.concatenate([cos, cos, rest], axis=1), jnp.concatenate([-sin, sin, rest], axis=1)


def solution(mesh):
    batch_axes = ('dp', AXIS)
    row_spec = P(AXIS, None)
    n_dev = mesh.shape[AXIS]
    chips = n_dev // 2
    n_off = chips - 1

    def device_step(tokens, embed_table, norm_attn, w_qkv, w_out, norm_mlp, w_gate_up, w_down, rope_scale):
        f32, bf16 = jnp.float32, jnp.bfloat16
        seq = tokens.shape[1]
        rows, d_model = w_out.shape
        head_dim = 2 * rope_scale.shape[0]
        q_width = rows * n_dev
        ff = w_gate_up.shape[1] // 2
        ffb = ff // chips
        lanes = 128
        tok = jnp.zeros((8, lanes), jnp.int32) + jnp.pad(tokens, ((0, 0), (0, lanes - seq)))
        column = lax.broadcasted_iota(jnp.int32, (rows, lanes), 1)
        gains = (jnp.where(column == head_dim, norm_attn[:, None], 0)
                 + jnp.where(column == head_dim + 1, norm_mlp[:, None], 0)).astype(bf16)
        cos2, sin2 = rope_tables(rope_scale, seq, lanes)
        vmem = pl.BlockSpec(memory_space=pltpu.VMEM)

        x_own, mine, wgu_all, wo_all, gain_rows = pl.pallas_call(
            front_kernel, name='front',
            out_shape=(jax.ShapeDtypeStruct((seq, d_model), bf16),
                       jax.ShapeDtypeStruct((chips, seq, 6 * lanes), bf16),
                       jax.ShapeDtypeStruct((chips, 2, rows, 2 * ffb), bf16),
                       jax.ShapeDtypeStruct((chips, 2, rows, d_model), bf16),
                       jax.ShapeDtypeStruct((8, d_model), f32)),
            in_specs=[ANY, vmem, vmem, vmem, vmem, ANY, ANY, ANY], out_specs=(vmem, ANY, ANY, ANY, vmem),
            scratch_shapes=[pltpu.VMEM((chips, 8, lanes), jnp.int32),
                            pltpu.VMEM((chips * seq, 1), f32),
                            pltpu.VMEM((2,) + embed_table.shape, bf16),
                            pltpu.VMEM((2, 4 * seq, embed_table.shape[0]), bf16),
                            pltpu.VMEM((chips * seq, d_model), bf16),
                            pltpu.VMEM((seq, d_model * n_off), bf16),
                            pltpu.VMEM((chips * seq, d_model), bf16),
                            pltpu.VMEM((chips, rows, 6 * lanes), bf16),
                            pltpu.VMEM((d_model, 6 * lanes), bf16),
                            pltpu.VMEM((5 * seq, d_model), bf16),
                            pltpu.VMEM((5 * seq, 6 * lanes), f32),
                            pltpu.VMEM((chips, seq, 6 * lanes), bf16),
                            dma2(n_off + 1), dma2(n_off), dma2(n_off + 1), dma2(2 * n_off), dma2(n_off + 1),
                            dma2(AG_MSGS), dma2(chips), dma2(RS_MSGS), dma2(AG_MSGS), dma2(n_off), dma(6)],
            compiler_params=params(1),
        )(tok, gains, w_qkv, cos2, sin2, w_gate_up, w_out, embed_table)

        wo_full = wo_all.reshape(q_width, d_model)
        gain_mlp = gain_rows[1]
        heads = mine.reshape(chips, seq, 6, lanes)[..., :head_dim].transpose(2, 1, 0, 3)

        def by_head(i):
            return jnp.stack([heads[2 * i], heads[2 * i + 1]], axis=2).reshape(seq, 2 * chips, head_dim)

        ctx_own = by_head(0).reshape(seq, q_width)
        key_own = by_head(1)[None]
        val_own = by_head(2)[None]

        attn_proj = jnp.dot(ctx_own, wo_full, preferred_element_type=f32)
        x_mid = (x_own.astype(f32) + attn_proj).astype(bf16)
        normed_mlp = rms_norm(x_mid, gain_mlp)

        layer_out = pl.pallas_call(
            mlp_kernel, name='mlp',
            out_shape=jax.ShapeDtypeStruct((seq, d_model), bf16),
            in_specs=[ANY, vmem, ANY, ANY], out_specs=vmem,
            scratch_shapes=[pltpu.VMEM((chips * seq, d_model), bf16),
                            pltpu.VMEM((chips, 2, rows, 2 * ffb), bf16),
                            pltpu.VMEM((2, ffb // 2, d_model), bf16),
                            pltpu.VMEM((chips * seq, ffb), bf16),
                            pltpu.VMEM((chips * seq, d_model), f32),
                            pltpu.VMEM((seq, d_model * n_off), f32),
                            dma(AG_MSGS), dma(AG_MSGS), dma(RS_MSGS), dma(RS_MSGS), dma(1), dma(1), dma(3)],
            compiler_params=params(4),
        )(normed_mlp, x_mid, wgu_all, w_down)
        return layer_out[None], key_own, val_own

    return jax.shard_map(
        device_step,
        mesh=mesh,
        in_specs=(P(batch_axes, None), row_spec, P(AXIS), row_spec, row_spec, P(AXIS), row_spec, row_spec, P(None)),
        out_specs=(P(batch_axes, None, None), P(batch_axes, None, None, None), P(batch_axes, None, None, None)),
        check_vma=False,
    )
```

time: 442 us -> 359 us (0.81)
  matrix products: 43.1 us -> 8.43 us
  local copies, waits for them, and re-layouts: 34.1 us -> 9.7 us
  other arithmetic: 16.3 us -> 4.05 us
  Pallas kernels: 344 us -> 336 us
    dot_general x4 -> x0, matrix products: 28.2 us -> none  [the longest x2 26 us: pick(): return jnp.dot(hot, table, preferred_element_type=f32)]
    slice x7 -> x1, local copies, waits for them, and re-layouts: 11.5 us -> 0.91 us  [device_step(): gain_mlp = gain_rows[1]]
    pallas_call x3 -> x1, Pallas kernels: 234 us -> 225 us  [device_step(): pl.pallas_call(front_kernel, name='front', out_shape=(jax.ShapeDtypeStruc...]
    reshape x11 -> x1, local copies, waits for them, and re-layouts: 10.4 us -> 3.39 us  [device_step(): mine.reshape(chips, seq, 6, lanes)[..., :head_dim].transpose(2, 1, 0, 3)]
    convert_element_type x3 -> x1, other arithmetic: 6.68 us -> 0.9 us  [rms_norm(): return (h_f32 * inv_rms * gain.astype(jnp.float32)).astype(jnp.bfloat16)]
    slice x1 -> x0, matrix products: 5.04 us -> none  [device_step(): jnp.dot(normed, wq_own, preferred_element_type=f32)[:, :width]]
where the time goes in v3:
time: 359 us
  Pallas kernels  336 us (94%)
  local copies, waits for them, and re-layouts  9.7 us (3%)
  matrix products  8.43 us (2%)
  other arithmetic  4.05 us (1%)
    pallas_call x1, Pallas kernels, device_step(): pl.pallas_call(front_kernel, name='front', out_shape=(jax.ShapeDtypeStruc...  225 us
    pallas_call x1, Pallas kernels, device_step(): pl.pallas_call(mlp_kernel, name='mlp', out_shape=jax.ShapeDtypeStruct((se...  111 us
    dot_general x1, matrix products, device_step(): attn_proj = jnp.dot(ctx_own, wo_full, preferred_element_type=f32)  8.43 us

profile of v3, /device:TPU:96, one launch (start us, length us, event | category | flops | bytes accessed | tf_op | source)
XLA Modules:
  0.0 358.9 jit_solution(10442794395025260801)
XLA Ops:
  0.6 0.7 pad_bitcast_fusion
  1.3 0.7 multiply_divide_fusion
  2.0 0.1 pad.16.clone
  2.0 0.6 add.27.tok
  2.6 1.4 select_add_fusion.gains
  4.0 0.1 fusion.10
  4.2 0.7 maximum_maximum_fusion.1
  4.9 224.8 %front.1 = (bf16[64,3072]{1,0:T(8,128)(2,1)}, bf16[16,64,768]{2,1,0:T(8,128)(2,1)}, bf16[16,2,96,1024]{3,2,1,0:T(8,128)(2,1)}, bf16[16,2,96,3072]{3,2,1,0:T(8,128)(2,1)}, f32[8,3072]{1,0:T(8,128)}) custom-call(s32[8,128]{1,0:T(8,128)} %add.27.tok, bf16[96,128]{1,0:T(8,128)(2,1)} %select_add_fusion.gains, bf16[96,9216]{1,0:T(8,128)(2,1)} %wqkv.1, ...), custom_call_target="tpu_custom_call" | custom-call | tf_op jit(solution)/shard_map/front/pallas_call | solution.py:548
  229.7 0.9 slice.27
  230.6 3.4 reshape.21
  234.0 0.4 copy.23
  234.4 0.1 slice_bitcast_fusion.1
  234.6 0.4 copy-done.2
  235.0 8.4 %fusion.2 = (f32[64]{0:T(128)S(1)}, bf16[64,3072]{1,0:T(8,128)(2,1)S(1)}) fusion(bf16[16,2,96,3072]{3,2,1,0:T(8,128)(2,1)} %get-tuple-element.10, bf16[64,16,1,96]{3,0,2,1:T(8,128)(2,1)S(1)} %get-tuple-element.20, bf16[64,16,1,96]{3,0,2,1:T(8,128)(2,1)S(1)} %get-tuple-element.21, bf16[64,3072]{1,0:T(8,128)(2,1)S(1)} %copy-done.2), kind=kOutput, calls=%fused_computation.6 | convolution fusion | flops 1209335808 | bytes 20054272 | tf_op jit(solution)/shard_map/dot_general | solution.py:584
  243.4 0.0 copy-start
  243.5 0.1 pad_maximum_fusion.1
  243.6 1.1 copy.19
  244.8 0.9 fusion.4.h_own
  245.7 111.1 %mlp.1 = bf16[64,3072]{1,0:T(8,128)(2,1)} custom-call(bf16[64,3072]{1,0:T(8,128)(2,1)} %fusion.4.h_own, bf16[64,3072]{1,0:T(8,128)(2,1)} %copy-done, bf16[16,2,96,1024]{3,2,1,0:T(8,128)(2,1)} %get-tuple-element.12.wgu_hbm, bf16[256,3072]{1,0:T(8,128)(2,1)} %wd_hbm.1), custom_call_target="tpu_custom_call" | custom-call | tf_op jit(solution)/shard_map/mlp/pallas_call | solution.py:588
  356.8 0.0 copy-start.1
  356.8 0.1 pad_maximum_fusion
  357.0 1.1 copy.18
  358.1 0.0 copy-done.1
  358.1 0.7 copy.25
  (7 shorter events, 0.1 us)
Async XLA Ops:
  234.0 1.0 copy-start.2
  243.4 2.2 copy-start
  356.8 1.3 copy-start.1

commit v4 on v3

--- a/solution.py
+++ b/solution.py
@@ -135,11 +135,19 @@
             self.recv(h, '1mf')
             self.second(h, 2)
 
-    def run(self, hook=lambda first, n: None):
+    def rest(self, near=lambda: None, middle=lambda: None, before_last=lambda: None):
+        self.middle()
+        near()
+        self.second_forward(-1)
+        self.second_forward(1)
+        self.second_forward(2)
+        before_last()
+        middle()
+        for a in (0, -1, 1, 2):
+            self.last(a)
+
+    def run_slots(self, hook, before_last=lambda: None):
         self.begin()
-        self.rest(hook)
-
-    def rest(self, hook, before_last=lambda: None):
         self.middle()
         hook(0, 5)
         self.second_forward(-1)
@@ -154,6 +162,72 @@
         hook(11, 4)
         self.last(2)
         hook(15, 1)
+
+
+class Line:
+    STEPS = (0, 1, -1, 2)
+
+    def __init__(self, pos, m, name, axis):
+        self.pos, self.m, self.name, self.axis = pos, m, name, axis
+
+    def dev(self, t):
+        return self.pos.dev(0, t) if self.axis == 'x' else self.pos.dev(t, 0)
+
+    def index(self, t):
+        return lax.rem((self.pos.x if self.axis == 'x' else self.pos.y) + t + 4, 4)
+
+    def start(self, key, src, dst, t):
+        self.m.start((self.name, key), src, dst, self.dev(t))
+
+    def recv(self, key):
+        self.m.recv((self.name, key))
+
+    def gather_begin(self, buf):
+        self.start('gp', buf.at[0], buf.at[2], 1)
+        self.start('gm', buf.at[0], buf.at[1], -1)
+
+    def gather_forward(self, buf):
+        half = buf.shape[1] // 2
+        self.recv('gp')
+        self.start('gpf', buf.at[2, pl.ds(0, half)], buf.at[3, pl.ds(0, half)], 1)
+        self.recv('gm')
+        self.start('gmf', buf.at[1, pl.ds(half, half)], buf.at[3, pl.ds(half, half)], -1)
+
+    def gather_last(self):
+        self.recv('gpf')
+        self.recv('gmf')
+
+    def scatter_begin(self, part, recv_buf, rows):
+        half = part.shape[1] // 2
+        self.rows, self.half = rows, half
+        self.start('spf', part.at[self.block(2), pl.ds(0, half)], recv_buf.at[pl.ds(0, rows), pl.ds(0, half)], 1)
+        self.start('smf', part.at[self.block(2), pl.ds(half, half)], recv_buf.at[pl.ds(0, rows), pl.ds(half, half)], -1)
+
+    def block(self, t, lo=0, n=None):
+        return pl.ds(pl.multiple_of(self.index(t) * self.rows + lo, 16), self.rows if n is None else n)
+
+    def add(self, part, recv_buf, t, first, cols):
+        @pl.loop(0, self.rows // 16)
+        def _(i):
+            lo = pl.multiple_of(i * 16, 16)
+            mine = self.block(t, lo, 16)
+            part[mine, cols] = part[mine, cols] + recv_buf[pl.ds(pl.multiple_of(first + lo, 16), 16), cols]
+
+    def scatter_middle(self, part, recv_buf):
+        rows, half = self.rows, self.half
+        self.recv('spf')
+        self.add(part, recv_buf, 1, 0, pl.ds(0, half))
+        self.start('sp', part.at[self.block(1)], recv_buf.at[pl.ds(rows, rows)], 1)
+        self.recv('smf')
+        self.add(part, recv_buf, -1, 0, pl.ds(half, half))
+        self.start('sm', part.at[self.block(-1)], recv_buf.at[pl.ds(2 * rows, rows)], -1)
+
+    def scatter_last(self, part, recv_buf):
+        every = pl.ds(0, 2 * self.half)
+        self.recv('sp')
+        self.add(part, recv_buf, 0, self.rows, every)
+        self.recv('sm')
+        self.add(part, recv_buf, 0, 2 * self.rows, every)
 
 
 class Scatter:
@@ -235,15 +309,16 @@
 
 
 def front_kernel(tok, gains, wqkv, cos2, sin2, wgu, wo, table,
-                 x_own, mine, wgu_all, wo_all, gain_rows,
+                 x_mid, mine, wgu_all, gain_rows,
                  tok_all, tok_col, tbl, hot, part, recv_buf, x_all, wq_out, wq, normed, proj, packed,
-                 t_sem, q_sem, qf_sem, g_sem, gf_sem, o_sem, of_sem, r_sem, a_sem, e_sem, l_sem):
+                 ctx_x, ctx_y, wo_x, wo_y, sum_x, sum_y, got_x, got_y,
+                 t_sem, q_sem, qf_sem, g_sem, gf_sem, o_sem, of_sem, r_sem, a_sem, e_sem, c_sem, l_sem):
     f32, bf16 = jnp.float32, jnp.bfloat16
     pos = Place(4)
     offs = offsets(4)
     here = pos.chip(0, 0)
     rows, lanes = wq_out.shape[1], 128
-    seq, width = x_own.shape
+    seq, width = packed.shape[1], x_all.shape[1]
     n_slots = len(SLOTS)
     n_off = len(offs)
     ff = wgu.shape[1] // 2
@@ -252,8 +327,17 @@
     table_rows = table.shape[0]
     tile = 256
     loads = [pltpu.make_async_copy(table, tbl.at[pos.c], l_sem.at[0]),
-             pltpu.make_async_copy(tok, tok_all.at[0], l_sem.at[1]),
-             pltpu.make_async_copy(wo, wo_all.at[here, pos.c], l_sem.at[2])]
+             pltpu.make_async_copy(tok, tok_all.at[0], l_sem.at[1])]
+    colb = width // 4
+    my_head = pl.ds(pl.multiple_of(pos.c * lanes, lanes), rows)
+    m4 = Msgs(c_sem.at[0], c_sem.at[1])
+    line_x, line_y = Line(pos, m4, 'x', 'x'), Line(pos, m4, 'y', 'y')
+
+    def out_cols(line, t):
+        return wo.at[:, pl.ds(pl.multiple_of(line.index(t) * colb, lanes), colb)]
+
+    for k, (line, w) in enumerate(((line_x, wo_x), (line_y, wo_y))):
+        loads.append(pltpu.make_async_copy(out_cols(line, 0), w.at[0, my_head], l_sem.at[6 + k]))
     for j in (0, 1):
         src = wgu.at[:, pl.ds(pl.multiple_of(j * ff + here * ffb, 128), ffb)]
         loads.append(pltpu.make_async_copy(src, wgu_all.at[here, pos.c, :, pl.ds(j * ffb, ffb)], l_sem.at[3 + j]))
@@ -266,6 +350,10 @@
         cp.start()
     swap = remote(table, tbl.at[pos.c], t_sem, n_off, pos.partner)
     swap.start()
+    pad = jnp.zeros((4, lanes - rows, colb), bf16)
+    for w in (wo_x, wo_y):
+        for hd in (0, 1):
+            w[:, hd * lanes + rows:(hd + 1) * lanes, :] = pad
 
     for p in range(n_slots):
         for k in range(6):
@@ -279,6 +367,12 @@
     qs = [remote(wq_out.at[pos.chip(dy, dx)], wq.at[my_rows], q_sem, i, pos.dev(dy, dx)) for i, (dy, dx) in enumerate(offs)]
     for cp in qs:
         cp.start()
+    os = []
+    for k, (line, w) in enumerate(((line_x, wo_x), (line_y, wo_y))):
+        for i, t in enumerate((1, -1, 2)):
+            slot = Line.STEPS.index(2 if t == 2 else -t)
+            os.append(remote(out_cols(line, t), w.at[slot, my_head], o_sem, 3 * k + i, line.dev(t)))
+            os[-1].start()
     wq[my_rows, :] = wq_out[here]
 
     loads[1].wait()
@@ -337,7 +431,6 @@
 
     scatter.finish(send_gate_up)
     x_all[pl.ds(0, seq), :] = part[pl.ds(0, seq), :]
-    x_own[...] = part[pl.ds(0, seq), :]
 
     sends = []
 
@@ -362,95 +455,164 @@
             other = jnp.where(lane < head_dim // 2, pltpu.roll(u, lanes - head_dim // 2, 1), pltpu.roll(u, head_dim // 2, 1))
             return (u * cos2[...] + other * sin2[...]).astype(bf16)
 
-        @pl.loop(0, n)
-        def _(s):
-            mine_rows = pl.ds(pl.multiple_of(s * seq, seq), seq)
+        def one(s, seq_x, seq_y):
+            mine_rows = pl.ds(s * seq, seq)
+            kv = []
             for hd in (0, 1):
                 q = rope(proj[mine_rows, hd * lanes:(hd + 1) * lanes])
                 k = rope(proj[mine_rows, (2 + hd) * lanes:(3 + hd) * lanes])
-                v = proj[mine_rows, (4 + hd) * lanes:(5 + hd) * lanes].astype(bf16)
+                v = proj[mine_rows, (4 + hd) * lanes:(5 + hd) * lanes]
+                v = jnp.where(lane < head_dim, v, 0.0).astype(bf16)
                 scores = lax.dot_general(q, k, (((1,), (1,)), ((), ())), preferred_element_type=f32) * (head_dim ** -0.5)
                 scores = jnp.where(causal, scores, -jnp.inf)
                 e = jnp.exp(scores - jnp.max(scores, axis=-1, keepdims=True))
                 probs = (e / jnp.sum(e, axis=-1, keepdims=True)).astype(bf16)
                 context = jnp.dot(probs, v, preferred_element_type=f32).astype(bf16)
-                packed[first + s, :, hd * lanes:(hd + 1) * lanes] = context
-                packed[first + s, :, (2 + hd) * lanes:(3 + hd) * lanes] = k
-                packed[first + s, :, (4 + hd) * lanes:(5 + hd) * lanes] = v
-
-        for s in range(first, first + n):
-            if s == 0:
-                cp = pltpu.make_async_copy(packed.at[0], mine.at[here], l_sem.at[5])
-            else:
-                cp = remote(packed.at[s], mine.at[here], e_sem, s - 1, pos.dev(*SLOTS[s]))
-            cp.start()
-            sends.append(cp)
+                ctx_x[0, seq_x, hd * lanes:(hd + 1) * lanes] = context[:seq // 2]
+                ctx_y[0, seq_y, hd * lanes:(hd + 1) * lanes] = context[seq // 2:]
+                kv.append((k[:, :head_dim], v[:, :head_dim]))
+            packed[first + s] = jnp.concatenate([kv[0][0], kv[1][0], kv[0][1], kv[1][1]], axis=1)
+
+        half = seq // 2
+        for s in range(n):
+            a, b = SLOTS[first + s]
+            yq, xq = line_y.index(a), line_x.index(b)
+            one(s, pl.ds(pl.multiple_of((yq * 4 + xq) * half, half), half), pl.ds(pl.multiple_of((xq * 4 + yq) * half, half), half))
 
     m2 = Msgs(a_sem.at[0], a_sem.at[1])
     gather = Gather(pos, m2, lambda s, lo, n: x_all.at[pl.ds(s * seq, seq), pl.ds(lo, n)], width)
-    m3 = Msgs(o_sem.at[0], o_sem.at[1])
-    out_gather = Gather(pos, m3, lambda p, lo, n: wo_all.at[p, pos.c, :, pl.ds(lo, n)], width, by_chip=True)
     for cp in loads[2:]:
         cp.wait()
     forward(gf_sem, n_off, wgu_all.at[here, pos.c])
-    gather.begin()
-    gather.rest(attend, out_gather.begin)
-
-    def forward_out(first, n):
-        for s in range(first, first + n):
-            forward(of_sem, s, wo_all.at[pos.chip(*SLOTS[s]), pos.c])
+    o_fwd = [forward(of_sem, 4 * k, w.at[0, my_head]) for k, w in enumerate((wo_x, wo_y))]
+    for k, w in enumerate((wo_x, wo_y)):
+        for i, t in enumerate((1, -1, 2)):
+            os[3 * k + i].wait_recv()
+            slot = Line.STEPS.index(2 if t == 2 else -t)
+            o_fwd.append(forward(of_sem, 4 * k + slot, w.at[slot, my_head]))
+
+    gather.run_slots(attend)
+
+    lines = ((line_x, ctx_x, wo_x, sum_x, line_y, got_x), (line_y, ctx_y, wo_y, sum_y, line_x, got_y))
+    for line, ctx, *_ in lines:
+        line.gather_begin(ctx)
+    for s in range(n_slots):
+        if s == 0:
+            cp = pltpu.make_async_copy(packed.at[0], mine.at[here], l_sem.at[5])
+        else:
+            cp = remote(packed.at[s], mine.at[here], e_sem, s - 1, pos.dev(*SLOTS[s]))
+        sends.append(cp)
+    for line, ctx, *_ in lines:
+        line.gather_forward(ctx)
+    for cp in sends:
+        cp.start()
+    for cp in o_fwd:
+        cp.wait_recv()
+
+    def project(ctx, w, total, slots, add):
+        @pl.loop(0, colb // tile)
+        def _(i):
+            cols = pl.ds(pl.multiple_of(i * tile, tile), tile)
+            acc = sum(jnp.dot(ctx[j], w[j, :, cols], preferred_element_type=f32) for j in slots)
+            total[:, cols] = total[:, cols] + acc if add else acc
+
+    for line, ctx, w, total, *_ in lines:
+        project(ctx, w, total, (0, 1, 2), False)
+    for line, ctx, w, total, other, got in lines:
+        line.gather_last()
+        project(ctx, w, total, (3,), True)
+        other.scatter_begin(total, got, total.shape[0] // 4)
+    for line, ctx, w, total, other, got in lines:
+        other.scatter_middle(total, got)
+    half = seq // 2
+    for k, (line, ctx, w, total, other, got) in enumerate(lines):
+        other.scatter_last(total, got)
+        cols = pl.ds(pl.multiple_of(line.index(0) * colb, lanes), colb)
+        for t in Line.STEPS:
+            a, b = (0, t) if k == 0 else (t, 0)
+            x = x_all[pl.ds(slot_of(a, b) * seq + k * half, half), cols].astype(f32)
+            lo = pl.multiple_of(line.index(t) * half, half)
+            x_mid[k, pl.ds(lo, half), :] = (x + total[other.block(0, lo, half), :]).astype(bf16)
 
     for i, (dy, dx) in enumerate(offs):
         gs[2 * i].wait_recv()
         gs[2 * i + 1].wait_recv()
         forward(gf_sem, i, wgu_all.at[pos.chip(-dy, -dx), pos.c])
-    out_gather.rest(forward_out)
     for cp in sends:
         cp.wait()
-    for cp in toks + qs + gs + [swap]:
+    for cp in toks + qs + gs + os + [swap]:
         cp.wait_send()
-    for cp in fwd[:1 + n_off]:
-        cp.wait_send()
-    for cp in fwd[1 + n_off:]:
-        cp.wait()
-    for msgs in (m, m2, m3):
+    waited = q_fwd + o_fwd
+    for cp in fwd:
+        if any(cp is w for w in waited):
+            cp.wait_send()
+        else:
+            cp.wait()
+    for msgs in (m, m2, m4):
         msgs.drain()
 
 
-def mlp_kernel(h_own, x_mid, wgu_hbm, wd_hbm, out, h_all, wgu, wd, act, part, recv_buf,
+def mlp_kernel(piece, gain_rows, wgu_hbm, wd_hbm, out, mid_x, mid_y, normed, wgu, wd, act, part, recv_buf,
                s1, r1, s2, r2, w_send, w_recv, l_sem):
     pos = Place(4)
     f32, bf16 = jnp.float32, jnp.bfloat16
     rows, width = out.shape
+    half_rows = rows // 2
+    n_rows, colb = piece.shape[1:]
     ffb = act.shape[1]
     half = ffb // 2
     tile = 256
-    loads = [pltpu.make_async_copy(h_own, h_all.at[pl.ds(0, rows)], l_sem.at[0]),
+    m = Msgs(s1, r1)
+    line_x, line_y = Line(pos, m, 'x', 'x'), Line(pos, m, 'y', 'y')
+
+    def blk(p, lo, n):
+        y, x = lax.div(p, 4), lax.rem(p, 4)
+        first = lo < colb
+        r, c = (y, x) if first else (x, y)
+        ref = mid_x if first else mid_y
+        lo = lo if first else lo - colb
+        return ref.at[pl.ds(pl.multiple_of(r * n_rows, n_rows), n_rows), pl.ds(pl.multiple_of(c * colb + lo, 128), n)]
+
+    here = pos.chip(0, 0)
+    loads = [pltpu.make_async_copy(piece.at[0], blk(here, 0, colb), l_sem.at[0]),
+             pltpu.make_async_copy(piece.at[1], blk(here, colb, colb), l_sem.at[3]),
              pltpu.make_async_copy(wgu_hbm, wgu, l_sem.at[1]),
              pltpu.make_async_copy(wd_hbm, wd.at[pos.c], l_sem.at[2])]
     for cp in loads:
         cp.start()
     barrier(torus_neighbours(pos) + [pos.partner])
+    loads[0].wait()
+    loads[1].wait()
+    gather = Gather(pos, m, blk, 2 * colb, by_chip=True)
     push = pltpu.make_async_remote_copy(src_ref=wd_hbm, dst_ref=wd.at[pos.c], send_sem=w_send.at[0], recv_sem=w_recv.at[0],
                                         device_id={AXIS: pos.partner}, device_id_type=MESH)
     push.start()
-    loads[0].wait()
-    waited = []
-
-    def gate_up(first, n):
-        if not waited:
-            loads[1].wait()
-            waited.append(True)
-        mine = pl.ds(first * rows, n * rows)
+
+    def gate_up(v):
+        for k, (mid, line, other) in enumerate(((mid_x, line_y, line_x), (mid_y, line_x, line_y))):
+            for i, t in enumerate(Line.STEPS):
+                src = pl.multiple_of(line.index(v) * n_rows + other.index(t) * half_rows, half_rows)
+                dst = (k * 4 + i) * half_rows
+
+                @pl.loop(0, half_rows // 16)
+                def _(j):
+                    x = mid[pl.ds(pl.multiple_of(src + j * 16, 16), 16), :].astype(f32)
+                    inv = lax.rsqrt(jnp.mean(x * x, axis=-1, keepdims=True) + NORM_EPS)
+                    normed[pl.ds(pl.multiple_of(dst + j * 16, 16), 16), :] = (x * inv * gain_rows[1:2, :]).astype(bf16)
 
         @pl.loop(0, ffb // tile)
         def _(i):
             lo = pl.multiple_of(i * tile, tile)
-            h = h_all[mine, :]
+            h = normed[...]
             g = jnp.dot(h, wgu[:, :, :, pl.ds(lo, tile)].reshape(width, tile), preferred_element_type=f32)
             u = jnp.dot(h, wgu[:, :, :, pl.ds(pl.multiple_of(ffb + lo, tile), tile)].reshape(width, tile),
                         preferred_element_type=f32)
-            act[mine, pl.ds(lo, tile)] = (jax.nn.silu(g) * u).astype(bf16)
+            a = (jax.nn.silu(g) * u).astype(bf16)
+            for k in (0, 1):
+                for i, t in enumerate(Line.STEPS):
+                    slot = slot_of(v, t) if k == 0 else slot_of(t, v)
+                    src = (k * 4 + i) * half_rows
+                    act[pl.ds(slot * rows + k * half_rows, half_rows), pl.ds(lo, tile)] = a[src:src + half_rows]
 
     def down(first, n):
         mine = pl.ds(first * rows, n * rows)
@@ -460,9 +622,18 @@
             cols = pl.ds(pl.multiple_of(i * tile, tile), tile)
             part[mine, cols] = jnp.dot(act[mine, :], wd[:, :, cols].reshape(2 * half, tile), preferred_element_type=f32)
 
-    m = Msgs(s1, r1)
-    Gather(pos, m, lambda s, lo, n: h_all.at[pl.ds(s * rows, rows), pl.ds(lo, n)], width).run(gate_up)
-    loads[2].wait()
+    def near():
+        loads[2].wait()
+        gate_up(0)
+
+    def middle():
+        gate_up(1)
+        gate_up(-1)
+
+    gather.begin()
+    gather.rest(near, middle)
+    gate_up(2)
+    loads[3].wait()
     push.wait()
     m2 = Msgs(s2, r2)
     scatter = Scatter(pos, m2, part, recv_buf, rows, width)
@@ -470,30 +641,14 @@
     scatter.begin()
     down(0, 9)
     scatter.finish()
-    out[...] = (x_mid[...].astype(f32) + part[pl.ds(0, rows), :]).astype(bf16)
+    for k, (mid, line, other) in enumerate(((mid_x, line_y, line_x), (mid_y, line_x, line_y))):
+        src = pl.multiple_of(line.index(0) * n_rows + other.index(0) * half_rows, half_rows)
+        mine = pl.ds(k * half_rows, half_rows)
+        out[mine, :] = (mid[pl.ds(src, half_rows), :].astype(f32) + part[mine, :]).astype(bf16)
     m.drain()
     m2.drain()
 
 
-def exchange_kernel(side, src, dst, sems, recvs, l_sem):
-    pos = Place(side)
-    offs = offsets(side)
-    me_chip = pos.chip(0, 0)
-    barrier([pos.dev(dy, dx) for dy, dx in offs])
-    copies = []
-    for i, (dy, dx) in enumerate(offs):
-        cp = pltpu.make_async_remote_copy(
-            src_ref=src.at[pos.chip(dy, dx)], dst_ref=dst.at[me_chip], send_sem=sems.at[i], recv_sem=recvs.at[i],
-            device_id={AXIS: pos.dev(dy, dx)}, device_id_type=MESH)
-        cp.start()
-        copies.append(cp)
-    own = pltpu.make_async_copy(src.at[me_chip], dst.at[me_chip], l_sem.at[0])
-    own.start()
-    own.wait()
-    for cp in copies:
-        cp.wait()
-
-
 def dma(n):
     return pltpu.SemaphoreType.DMA((n,))
 
@@ -504,12 +659,6 @@
 
 def params(cid):
     return pltpu.CompilerParams(collective_id=cid, has_side_effects=True, vmem_limit_bytes=VMEM_LIMIT)
-
-
-def rms_norm(hidden, gain):
-    h_f32 = hidden.astype(jnp.float32)
-    inv_rms = lax.rsqrt(jnp.mean(h_f32 * h_f32, axis=-1, keepdims=True) + NORM_EPS)
-    return (h_f32 * inv_rms * gain.astype(jnp.float32)).astype(jnp.bfloat16)
 
 
 def rope_tables(rope_scale, seq_len, lanes):
@@ -545,14 +694,15 @@
         cos2, sin2 = rope_tables(rope_scale, seq, lanes)
         vmem = pl.BlockSpec(memory_space=pltpu.VMEM)
 
-        x_own, mine, wgu_all, wo_all, gain_rows = pl.pallas_call(
+        half_toks = chips * seq // 2
+        colb = d_model // 4
+        x_mid, mine, wgu_all, gain_rows = pl.pallas_call(
             front_kernel, name='front',
-            out_shape=(jax.ShapeDtypeStruct((seq, d_model), bf16),
-                       jax.ShapeDtypeStruct((chips, seq, 6 * lanes), bf16),
+            out_shape=(jax.ShapeDtypeStruct((2, half_toks // 4, colb), bf16),
+                       jax.ShapeDtypeStruct((chips, seq, 4 * head_dim), bf16),
                        jax.ShapeDtypeStruct((chips, 2, rows, 2 * ffb), bf16),
-                       jax.ShapeDtypeStruct((chips, 2, rows, d_model), bf16),
                        jax.ShapeDtypeStruct((8, d_model), f32)),
-            in_specs=[ANY, vmem, vmem, vmem, vmem, ANY, ANY, ANY], out_specs=(vmem, ANY, ANY, ANY, vmem),
+            in_specs=[ANY, vmem, vmem, vmem, vmem, ANY, ANY, ANY], out_specs=(vmem, ANY, ANY, vmem),
             scratch_shapes=[pltpu.VMEM((chips, 8, lanes), jnp.int32),
                             pltpu.VMEM((chips * seq, 1), f32),
                             pltpu.VMEM((2,) + embed_table.shape, bf16),
@@ -564,40 +714,34 @@
                             pltpu.VMEM((d_model, 6 * lanes), bf16),
                             pltpu.VMEM((5 * seq, d_model), bf16),
                             pltpu.VMEM((5 * seq, 6 * lanes), f32),
-                            pltpu.VMEM((chips, seq, 6 * lanes), bf16),
-                            dma2(n_off + 1), dma2(n_off), dma2(n_off + 1), dma2(2 * n_off), dma2(n_off + 1),
-                            dma2(AG_MSGS), dma2(chips), dma2(RS_MSGS), dma2(AG_MSGS), dma2(n_off), dma(6)],
+                            pltpu.VMEM((chips, seq, 4 * head_dim), bf16)]
+                           + [pltpu.VMEM((4, half_toks, 2 * lanes), bf16)] * 2
+                           + [pltpu.VMEM((4, 2 * lanes, colb), bf16)] * 2
+                           + [pltpu.VMEM((half_toks, colb), f32)] * 2
+                           + [pltpu.VMEM((3 * half_toks // 4, colb), f32)] * 2
+                           + [dma2(n_off + 1), dma2(n_off), dma2(n_off + 1), dma2(2 * n_off), dma2(n_off + 1),
+                              dma2(6), dma2(8), dma2(RS_MSGS), dma2(AG_MSGS), dma2(n_off), dma2(16), dma(8)],
             compiler_params=params(1),
         )(tok, gains, w_qkv, cos2, sin2, w_gate_up, w_out, embed_table)
-
-        wo_full = wo_all.reshape(q_width, d_model)
-        gain_mlp = gain_rows[1]
-        heads = mine.reshape(chips, seq, 6, lanes)[..., :head_dim].transpose(2, 1, 0, 3)
-
-        def by_head(i):
-            return jnp.stack([heads[2 * i], heads[2 * i + 1]], axis=2).reshape(seq, 2 * chips, head_dim)
-
-        ctx_own = by_head(0).reshape(seq, q_width)
-        key_own = by_head(1)[None]
-        val_own = by_head(2)[None]
-
-        attn_proj = jnp.dot(ctx_own, wo_full, preferred_element_type=f32)
-        x_mid = (x_own.astype(f32) + attn_proj).astype(bf16)
-        normed_mlp = rms_norm(x_mid, gain_mlp)
 
         layer_out = pl.pallas_call(
             mlp_kernel, name='mlp',
             out_shape=jax.ShapeDtypeStruct((seq, d_model), bf16),
             in_specs=[ANY, vmem, ANY, ANY], out_specs=vmem,
-            scratch_shapes=[pltpu.VMEM((chips * seq, d_model), bf16),
+            scratch_shapes=[pltpu.VMEM((half_toks, d_model), bf16),
+                            pltpu.VMEM((half_toks, d_model), bf16),
+                            pltpu.VMEM((half_toks // 2, d_model), bf16),
                             pltpu.VMEM((chips, 2, rows, 2 * ffb), bf16),
                             pltpu.VMEM((2, ffb // 2, d_model), bf16),
                             pltpu.VMEM((chips * seq, ffb), bf16),
                             pltpu.VMEM((chips * seq, d_model), f32),
                             pltpu.VMEM((seq, d_model * n_off), f32),
-                            dma(AG_MSGS), dma(AG_MSGS), dma(RS_MSGS), dma(RS_MSGS), dma(1), dma(1), dma(3)],
+                            dma(AG_MSGS), dma(AG_MSGS), dma(RS_MSGS), dma(RS_MSGS), dma(1), dma(1), dma(4)],
             compiler_params=params(4),
-        )(normed_mlp, x_mid, wgu_all, w_down)
+        )(x_mid, gain_rows, wgu_all, w_down)
+
+        heads = mine.reshape(chips, seq, 2, 2, head_dim).transpose(2, 1, 0, 3, 4).reshape(2, 1, seq, 2 * chips, head_dim)
+        key_own, val_own = heads[0], heads[1]
         return layer_out[None], key_own, val_own
 
     return jax.shard_map(

time: 359 us -> 333 us (0.928)
  Pallas kernels: 336 us -> 323 us
  matrix products: 8.43 us -> 0 us
  local copies, waits for them, and re-layouts: 9.7 us -> 6.1 us
    pallas_call x1, Pallas kernels: 225 us -> 208 us  [device_step(): pl.pallas_call(front_kernel, name='front', out_shape=(jax.ShapeDtypeStruc...]
    dot_general x1 -> x0, matrix products: 8.43 us -> none  [device_step(): attn_proj = jnp.dot(ctx_own, wo_full, preferred_element_type=f32)]
    pallas_call x1, Pallas kernels: 111 us -> 116 us  [device_step(): pl.pallas_call(mlp_kernel, name='mlp', out_shape=jax.ShapeDtypeStruct((se...]
where the time goes in v4:
time: 333 us
  Pallas kernels  323 us (97%)
  local copies, waits for them, and re-layouts  6.1 us (2%)
    pallas_call x1, Pallas kernels, device_step(): pl.pallas_call(front_kernel, name='front', out_shape=(jax.ShapeDtypeStruc...  208 us
    pallas_call x1, Pallas kernels, device_step(): pl.pallas_call(mlp_kernel, name='mlp', out_shape=jax.ShapeDtypeStruct((se...  116 us

profile of v4, /device:TPU:96, one launch (start us, length us, event | category | flops | bytes accessed | tf_op | source)
XLA Modules:
  0.0 333.2 jit_solution(18079292467274590664)
XLA Ops:
  0.6 0.7 pad_bitcast_fusion
  1.3 0.7 multiply_divide_fusion
  2.0 0.1 pad.10.clone
  2.0 0.6 add.13.tok
  2.6 1.4 select_add_fusion.gains
  4.0 0.1 fusion.2
  4.2 0.7 maximum_maximum_fusion.1
  4.9 207.8 %front.1 = (bf16[2,128,768]{2,1,0:T(8,128)(2,1)}, bf16[16,64,384]{2,1,0:T(8,128)(2,1)}, bf16[16,2,96,1024]{3,2,1,0:T(8,128)(2,1)}, f32[8,3072]{1,0:T(8,128)}) custom-call(s32[8,128]{1,0:T(8,128)} %add.13.tok, bf16[96,128]{1,0:T(8,128)(2,1)} %select_add_fusion.gains, bf16[96,9216]{1,0:T(8,128)(2,1)} %wqkv.1, f32[64,128]{1,0:T(8,128)} %get-tuple-element.14.cos2, ...), custom_call_target="tpu_custom_call" | custom-call | tf_op jit(solution)/shard_map/front/pallas_call | solution.py:699
  212.7 0.0 copy-start.1
  212.7 115.6 %mlp.1 = bf16[64,3072]{1,0:T(8,128)(2,1)} custom-call(bf16[2,128,768]{2,1,0:T(8,128)(2,1)} %get-tuple-element.7.piece, f32[8,3072]{1,0:T(8,128)} %get-tuple-element.8.gain_rows, bf16[16,2,96,1024]{3,2,1,0:T(8,128)(2,1)} %get-tuple-element.9.wgu_hbm, bf16[256,3072]{1,0:T(8,128)(2,1)} %wd_hbm.1), custom_call_target="tpu_custom_call" | custom-call | tf_op jit(solution)/shard_map/mlp/pallas_call | solution.py:727
  328.4 0.0 copy-start
  328.4 0.0 copy-done.1
  328.4 0.6 reshape.17
  329.0 1.1 fusion.3
  330.1 1.2 copy.13
  331.3 1.2 copy.12
  332.4 0.0 copy-done
  332.4 0.7 copy.15
  (2 shorter events, 0.0 us)
Async XLA Ops:
  212.7 115.7 %copy-start.1 = (bf16[16,64,384]{2,1,0:T(8,128)(2,1)S(1)}, bf16[16,64,384]{2,1,0:T(8,128)(2,1)}, u32[]{:S(2)}) copy-start(bf16[16,64,384]{2,1,0:T(8,128)(2,1)} %get-tuple-element.10) | copy-start | bytes 2359300
  328.4 4.1 %copy-start = (bf16[64,3072]{1,0:T(8,128)(2,1)S(1)}, bf16[64,3072]{1,0:T(8,128)(2,1)}, u32[]{:S(2)}) copy-start(bf16[64,3072]{1,0:T(8,128)(2,1)} %mlp.1) | copy-start | bytes 1179652

commit v5 on v0

v5 whole, which is shorter than its diff:
```python
import jax
import jax.numpy as jnp
from jax import lax
from jax.experimental import pallas as pl
from jax.experimental.pallas import tpu as pltpu
from jax.sharding import PartitionSpec as P

NORM_EPS = 1e-5
ROPE_THETA = 10000.0
AXIS = 'fsdp'
MESH = pl.DeviceIdType.MESH
ANY = pl.BlockSpec(memory_space=pl.ANY)
VMEM_LIMIT = 60 * 1024 * 1024


class Place:
    def __init__(self, side):
        me = lax.axis_index(AXIS)
        self.side = side
        self.c = lax.rem(me, 2)
        chip = lax.div(me, 2)
        self.y = lax.div(chip, side)
        self.x = lax.rem(chip, side)
        self.me = me
        self.partner = me + 1 - 2 * self.c

    def chip(self, dy, dx):
        s = self.side
        return lax.rem(self.y + dy + s, s) * s + lax.rem(self.x + dx + s, s)

    def dev(self, dy, dx):
        return self.chip(dy, dx) * 2 + self.c


def barrier(devices):
    sem = pltpu.get_barrier_semaphore()
    for d in devices:
        pl.semaphore_signal(sem, inc=1, device_id={AXIS: d}, device_id_type=MESH)
    pl.semaphore_wait(sem, len(devices))


def remote(src, dst, sems, i, dev):
    send, recv = (sems.at[k, i] for k in (0, 1))
    return pltpu.make_async_remote_copy(src_ref=src, dst_ref=dst, send_sem=send, recv_sem=recv,
                                        device_id={AXIS: dev}, device_id_type=MESH)


class Msgs:
    def __init__(self, sems):
        self.sems, self.copies, self.received = sems, {}, set()

    def start(self, name, src, dst, dev):
        assert name not in self.copies
        self.copies[name] = remote(src, dst, self.sems, len(self.copies), dev)
        self.copies[name].start()

    def recv(self, name):
        self.received.add(name)
        self.copies[name].wait_recv()

    def finish(self):
        for name in self.copies:
            if name not in self.received:
                self.recv(name)
            self.copies[name].wait_send()


class Local:
    def __init__(self, sems):
        self.sems, self.copies = sems, {}

    def start(self, name, src, dst):
        self.copies[name] = pltpu.make_async_copy(src, dst, self.sems.at[len(self.copies)])
        self.copies[name].start()

    def wait(self, *names):
        for name in names:
            self.copies[name].wait()


STEPS = (0, 1, -1, 2)
AWAY = STEPS[1:]
SLOTS = sorted(((a, b) for a in STEPS for b in STEPS), key=lambda o: (2 in o, abs(o[0]) + abs(o[1])))


def slot_of(a, b):
    return SLOTS.index(((a + 1) % 4 - 1, (b + 1) % 4 - 1))


def slot_back(t):
    return STEPS.index(2 if t == 2 else -t)


def swap_if(h, a, b):
    return (b, a) if h == 0 else (a, b)


HALVES = (0, 1)
SIGNS = (1, -1)
LANES = 128
CHUNK = 16


def whole(n):
    return 0, n


def part_for(sign):
    return lambda n: (0 if sign > 0 else n // 2, n // 2)


def chunk(i, base=0):
    return pl.ds(pl.multiple_of(base + i * CHUNK, CHUNK), CHUNK)


class Gather:
    def __init__(self, pos, m, blk, width, by_chip=False):
        self.pos, self.m, self.blk, self.half, self.by_chip = pos, m, blk, width // 2, by_chip

    def send(self, h, name, a, b, cut, ta, tb):
        lo, n = cut(self.half)
        lo += self.half * h
        if self.by_chip:
            src = dst = self.blk(self.pos.chip(*swap_if(h, a, b)), lo, n)
        else:
            src = self.blk(slot_of(*swap_if(h, a, b)), lo, n)
            dst = self.blk(slot_of(*swap_if(h, a - ta, b - tb)), lo, n)
        self.m.start((h,) + name, src, dst, self.pos.dev(*swap_if(h, ta, tb)))

    def second(self, h, a):
        for sign in SIGNS:
            self.send(h, ('second', sign, a), a, 0, whole, 0, sign)

    def second_forward(self, a):
        for h in HALVES:
            for sign in SIGNS:
                self.m.recv((h, 'second', sign, a))
                self.send(h, ('second on', sign, a), a, -sign, part_for(sign), 0, sign)

    def last(self, a):
        for h in HALVES:
            for sign in SIGNS:
                self.m.recv((h, 'second on', sign, a))

    def begin(self):
        for h in HALVES:
            for sign in SIGNS:
                self.send(h, ('first', sign), 0, 0, whole, sign, 0)
        for h in HALVES:
            self.second(h, 0)
        for sign in SIGNS:
            for h in HALVES:
                self.m.recv((h, 'first', sign))
                self.send(h, ('first on', sign), -sign, 0, part_for(sign), sign, 0)
                self.second(h, -sign)
        self.second_forward(0)
        for h in HALVES:
            for sign in SIGNS:
                self.m.recv((h, 'first on', sign))
            self.second(h, 2)

    def forward(self):
        for a in AWAY:
            self.second_forward(a)


class Scatter:
    def __init__(self, pos, m, part, recv_buf, rows, width):
        self.pos, self.m, self.part, self.recv_buf = pos, m, part, recv_buf
        self.rows, self.half, self.used, self.places = rows, width // 2, 0, {}

    def send(self, h, name, a, b, cut, ta, tb):
        lo, n = cut(self.half)
        key = (h,) + name
        there = self.places[key] = pl.ds(self.used, n)
        self.used += n
        src = self.part.at[pl.ds(slot_of(*swap_if(1 - h, a, b)) * self.rows, self.rows), pl.ds(self.half * h + lo, n)]
        self.m.start(key, src, self.recv_buf.at[:, there], self.pos.dev(*swap_if(1 - h, ta, tb)))

    def recv_add(self, h, name, a, b, cut):
        lo, n = cut(self.half)
        key = (h,) + name
        self.m.recv(key)
        there, here = self.places[key], pl.ds(self.half * h + lo, n)
        base = slot_of(*swap_if(1 - h, a, b)) * self.rows

        @pl.loop(0, self.rows // CHUNK)
        def _(i):
            mine, theirs = chunk(i, base), chunk(i)
            self.part[mine, here] = self.part[mine, here] + self.recv_buf[theirs, there]

    def begin(self):
        for b in AWAY[::-1] + (0,):
            for h in HALVES:
                for sign in SIGNS:
                    self.send(h, ('first on', sign, b), 2, b, part_for(sign), sign, 0)

    def finish(self, hook):
        calls = iter(range(len(SLOTS)))
        order = AWAY[::-1] + (0,)
        for b in order:
            for h in HALVES:
                for sign in SIGNS:
                    self.recv_add(h, ('first on', sign, b), sign, b, part_for(sign))
                    self.send(h, ('first', sign, b), sign, b, whole, sign, 0)
                hook(next(calls))
        for b in order:
            for h in HALVES:
                for sign in SIGNS:
                    self.recv_add(h, ('first', sign, b), 0, b, whole)
                if b == 2:
                    for sign in SIGNS:
                        self.send(h, ('second on', sign), 0, b, part_for(sign), 0, sign)
                elif b == 0:
                    for sign in SIGNS:
                        self.recv_add(h, ('second', sign), 0, b, whole)
                else:
                    self.recv_add(h, ('second on', b), 0, b, part_for(b))
                    self.send(h, ('second', b), 0, b, whole, 0, b)
                hook(next(calls))


class Line:
    def __init__(self, pos, m, axis):
        self.pos, self.m, self.axis = pos, m, axis

    def dev(self, t):
        return self.pos.dev(0, t) if self.axis == 'x' else self.pos.dev(t, 0)

    def index(self, t):
        side = self.pos.side
        return lax.rem((self.pos.x if self.axis == 'x' else self.pos.y) + t + side, side)

    def block(self, t, n, lo=0, size=None):
        return pl.ds(pl.multiple_of(self.index(t) * n + lo, CHUNK), n if size is None else size)

    def lanes(self, t, n):
        return pl.ds(pl.multiple_of(self.index(t) * n, LANES), n)

    def start(self, key, src, dst, t):
        self.m.start((self.axis,) + key, src, dst, self.dev(t))

    def recv(self, *key):
        self.m.recv((self.axis,) + key)

    def share(self, buf, v, rows):
        for sign in SIGNS:
            self.start(('share', sign, v), buf.at[0, rows], buf.at[slot_back(sign), rows], sign)

    def share_on(self, buf, v, rows_of):
        for sign in SIGNS:
            self.recv('share', sign, v)
            rows = rows_of(part_for(sign))
            self.start(('share on', sign, v), buf.at[slot_back(sign), rows], buf.at[slot_back(2), rows], sign)

    def share_last(self, v):
        for sign in SIGNS:
            self.recv('share on', sign, v)

    def scatter_begin(self, part, recv_buf, rows):
        for sign in SIGNS:
            cols = pl.ds(*part_for(sign)(part.shape[1]))
            self.start(('sum on', sign), part.at[self.block(2, rows), cols], recv_buf.at[pl.ds(0, rows), cols], sign)

    def add(self, part, recv_buf, t, rows, first, cols):
        @pl.loop(0, rows // CHUNK)
        def _(i):
            mine = self.block(t, rows, i * CHUNK, CHUNK)
            part[mine, cols] = part[mine, cols] + recv_buf[chunk(i, first * rows), cols]

    def scatter_middle(self, part, recv_buf, rows):
        for sign in SIGNS:
            self.recv('sum on', sign)
            self.add(part, recv_buf, sign, rows, 0, pl.ds(*part_for(sign)(part.shape[1])))
            to = recv_buf.at[pl.ds(slot_back(sign) * rows, rows)]
            self.start(('sum', sign), part.at[self.block(sign, rows)], to, sign)

    def scatter_last(self, part, recv_buf, rows):
        for sign in SIGNS:
            self.recv('sum', sign)
            self.add(part, recv_buf, 0, rows, slot_back(sign), pl.ds(*whole(part.shape[1])))


def offsets():
    return SLOTS[5:9] + SLOTS[1:5] + SLOTS[15:] + SLOTS[9:15]


def norm_rows(x, gain):
    inv = lax.rsqrt(jnp.mean(x * x, axis=-1, keepdims=True) + NORM_EPS)
    return (x * inv * gain).astype(jnp.bfloat16)


def tiles(n, tile=256):
    return [(lo, min(tile, n - lo)) for lo in range(0, n, tile)]


def tile_of(i, base=0, tile=256):
    return pl.ds(pl.multiple_of(base + i * tile, LANES), tile)


def front_kernel(tok, gains, wqkv, cos2, sin2, wgu, wo, wd, table,
                 x_mid, mine, wgu_all, wd_x, wd_y, gain_rows,
                 packed, tok_all, tok_col, tbl, hot, part, recv_buf, h_all, wq_out, wq, x_parts, proj,
                 ctx_x, ctx_y, wo_x, wo_y, sum_x, sum_y, got_x, got_y, sems, l_sem):
    f32, bf16 = jnp.float32, jnp.bfloat16
    pos = Place(4)
    m, local = Msgs(sems), Local(l_sem)
    line_x, line_y = Line(pos, m, 'x'), Line(pos, m, 'y')
    offs = offsets()
    here = pos.chip(0, 0)
    rows = wq_out.shape[1]
    seq, width = packed.shape[1], h_all.shape[1]
    n_slots = len(SLOTS)
    half, colb = seq // 2, width // 4
    ffb = wgu_all.shape[-1] // 2
    head_dim = packed.shape[2] // 4
    table_rows = table.shape[0]
    my_head = pl.ds(pl.multiple_of(pos.c * LANES, LANES), rows)
    my_rows = pl.ds(pl.multiple_of(pos.me * rows, CHUNK), rows)
    lines = ((line_x, ctx_x, wo_x, sum_x, line_y, got_x), (line_y, ctx_y, wo_y, sum_y, line_x, got_y))
    downs = ((line_x, wd_x), (line_y, wd_y))

    def cols_of(w, line, t):
        return w.at[:, line.lanes(t, colb)]

    def gate_up_block(j, chip):
        return wgu.at[:, pl.ds(pl.multiple_of((j * n_slots + chip) * ffb, LANES), ffb)]

    def gate_up_place(j):
        return wgu_all.at[here, pos.c, :, pl.ds(j * ffb, ffb)]

    local.start('table', table, tbl.at[pos.c])
    local.start('tok', tok, tok_all.at[0])
    for k, (line, ctx, w, *_) in enumerate(lines):
        local.start(('wo', k), cols_of(wo, line, 0), w.at[0, my_head])
    for k, (line, w) in enumerate(downs):
        local.start(('wd', k), cols_of(wd, line, 0), w.at[0, pos.c])
    for j in HALVES:
        local.start(('wgu', j), gate_up_block(j, here), gate_up_place(j))
    barrier([pos.dev(*o) for o in offs] + [pos.partner])

    for o in offs:
        m.start(('tok', o), tok, tok_all.at[slot_of(-o[0], -o[1])], pos.dev(*o))
    m.start('table', table, tbl.at[pos.c], pos.partner)
    to_send = list(offs)

    def send_gate_up(n):
        for _ in range(min(n, len(to_send))):
            o = to_send.pop(0)
            for j in HALVES:
                m.start(('wgu', j, o), gate_up_block(j, pos.chip(*o)), gate_up_place(j), pos.dev(*o))

    send_gate_up(3)
    blank = jnp.zeros((len(STEPS), LANES - rows, colb), bf16)
    for w in (wo_x, wo_y):
        for hd in HALVES:
            w[:, hd * LANES + rows:(hd + 1) * LANES, :] = blank
    block = 2 * head_dim
    for p in range(n_slots):
        pieces = [wqkv[:, (j * n_slots + p) * block:(j * n_slots + p + 1) * block] for j in range(3)]
        wq_out[p] = jnp.concatenate(pieces + [gains[...]], axis=1)
    for o in offs:
        m.start(('wq', o), wq_out.at[pos.chip(*o)], wq.at[my_rows], pos.dev(*o))
    for k, (line, ctx, w, *_) in enumerate(lines):
        for t in AWAY:
            m.start(('wo', k, t), cols_of(wo, line, t), w.at[slot_back(t), my_head], line.dev(t))
    wq[my_rows, :] = wq_out[here]

    local.wait('tok')
    for o in offs:
        m.recv(('tok', o))
    for s in range(n_slots):
        column = jnp.transpose(tok_all[s].astype(f32))
        tok_col[pl.ds(s * seq, seq), :] = column[:seq, 0:1]
    local.wait('table')
    m.recv('table')
    group = hot.shape[1]
    for g in range(n_slots * seq // group):
        mine_rows = pl.ds(g * group, group)
        for cc in HALVES:
            ids = lax.broadcasted_iota(jnp.int32, (group, table_rows), 1) + (here * 2 + cc) * table_rows
            hot[cc] = jnp.where(tok_col[mine_rows, :] == ids.astype(f32), 1.0, 0.0).astype(bf16)

        @pl.loop(0, len(tiles(width)))
        def _(i):
            cols = tile_of(i)
            part[mine_rows, cols] = sum(jnp.dot(hot[cc], tbl[cc, :, cols], preferred_element_type=f32)
                                        for cc in HALVES).astype(bf16)

    scatter = Scatter(pos, m, part, recv_buf, seq, width)
    scatter.begin()

    def forward(name, ref):
        m.start(('to partner', name), ref, ref, pos.partner)

    forward(('wq', 0), wq.at[my_rows])
    for o in offs:
        m.recv(('wq', o))
        forward(('wq', o), wq.at[pl.ds(pl.multiple_of(pos.dev(-o[0], -o[1]) * rows, CHUNK), rows)])
    for o in [0] + offs:
        m.recv(('to partner', ('wq', o)))
    qkv_width = 3 * block
    for lo, n in tiles(width, LANES):
        square = jnp.transpose(wq[pl.ds(lo, n), qkv_width // LANES * LANES:].astype(f32))
        gain_rows[:, lo:lo + n] = square[qkv_width % LANES:qkv_width % LANES + gain_rows.shape[0], :]

    scatter.finish(lambda i: send_gate_up(1 if 5 < i < 14 else 0))

    @pl.loop(0, seq // CHUNK)
    def _(i):
        h_all[chunk(i), :] = norm_rows(part[chunk(i), :].astype(f32), gain_rows[0:1, :])

    def attend(first, n):
        for lo, size in tiles(proj.shape[1]):
            proj[pl.ds(0, n * seq), lo:lo + size] = jnp.dot(
                h_all[pl.ds(first * seq, n * seq), :], wq[:, lo:lo + size], preferred_element_type=f32)
        lane = lax.broadcasted_iota(jnp.int32, (seq, LANES), 1)
        causal = lax.broadcasted_iota(jnp.int32, (seq, seq), 0) >= lax.broadcasted_iota(jnp.int32, (seq, seq), 1)
        turn = head_dim // 2

        def wide(u):
            return jnp.concatenate([u, jnp.zeros((seq, LANES - head_dim), u.dtype)], axis=1)

        def rope(u):
            u = wide(u)
            other = jnp.where(lane < turn, pltpu.roll(u, LANES - turn, 1), pltpu.roll(u, turn, 1))
            return (u * cos2[...] + other * sin2[...]).astype(bf16)

        for lo, size in tiles(n, 2):
            heads = [(s, hd) for s in range(lo, lo + size) for hd in HALVES]

            def cut(s, j, hd):
                at = (2 * j + hd) * head_dim
                return proj[pl.ds(s * seq, seq), at:at + head_dim]

            q, k = ([rope(cut(s, j, hd)) for s, hd in heads] for j in HALVES)
            v = [cut(s, 2, hd).astype(bf16) for s, hd in heads]
            scores = [lax.dot_general(a, b, (((1,), (1,)), ((), ())), preferred_element_type=f32) for a, b in zip(q, k)]
            scores = [jnp.where(causal, u * (head_dim ** -0.5), -jnp.inf) for u in scores]
            e = [jnp.exp(u - jnp.max(u, axis=-1, keepdims=True)) for u in scores]
            probs = [(u / jnp.sum(u, axis=-1, keepdims=True)).astype(bf16) for u in e]
            context = [wide(jnp.dot(p, u, preferred_element_type=f32).astype(bf16)) for p, u in zip(probs, v)]
            for i, (s, hd) in enumerate(heads):
                a, b = SLOTS[first + s]
                yq, xq = line_y.index(a), line_x.index(b)
                at = slice(hd * LANES, (hd + 1) * LANES)
                ctx_x[0, pl.ds(pl.multiple_of((yq * pos.side + xq) * half, half), half), at] = context[i][:half]
                ctx_y[0, pl.ds(pl.multiple_of((xq * pos.side + yq) * half, half), half), at] = context[i][half:]
                if hd == 1:
                    pair = [u[:, :head_dim] for u in k[i - 1:i + 1] + v[i - 1:i + 1]]
                    packed[first + s] = jnp.concatenate(pair, axis=1)

    gather = Gather(pos, m, lambda s, lo, n: h_all.at[pl.ds(s * seq, seq), pl.ds(lo, n)], width)
    local.wait(*[(name, k) for name in ('wo', 'wd', 'wgu') for k in HALVES])
    forward('wgu', wgu_all.at[here, pos.c])
    for k, (line, ctx, w, *_) in enumerate(lines):
        forward(('wo', k, 0), w.at[0, my_head])
        forward(('wd', k, 0), downs[k][1].at[0, pos.c])
        for t in AWAY:
            m.recv(('wo', k, t))
            forward(('wo', k, t), w.at[slot_back(t), my_head])

    arrived = list(offs)

    def forward_gate_up(n):
        for _ in range(min(n, len(arrived))):
            o = arrived.pop(0)
            for j in HALVES:
                m.recv(('wgu', j, o))
            forward(('wgu', o), wgu_all.at[pos.chip(-o[0], -o[1]), pos.c])

    gather.begin()
    attend(0, 5)
    for a in (-1, 1):
        gather.second_forward(a)
    attend(5, 4)
    forward_gate_up(n_slots - 1 - len(to_send))
    gather.second_forward(2)
    for k, line in enumerate((line_x, line_y)):
        for t in AWAY:
            m.start(('x', k, t), part.at[pl.ds(k * half, half), line.lanes(t, colb)], x_parts.at[k, slot_back(t)], line.dev(t))
        x_parts[k, 0] = part[pl.ds(k * half, half), line.lanes(0, colb)]
    send_gate_up(n_slots)
    gather.last(0)
    attend(9, 2)
    for a in (-1, 1):
        gather.last(a)
    attend(11, 4)
    gather.last(2)
    attend(15, 1)

    every = pl.ds(*whole(ctx_x.shape[1]))
    for line, ctx, *_ in lines:
        line.share(ctx, 'ctx', every)
    for line, ctx, *_ in lines:
        line.share_on(ctx, 'ctx', lambda cut: pl.ds(*cut(ctx_x.shape[1])))

    def send_kv():
        local.start('kv', packed.at[0], mine.at[here])
        for s, o in enumerate(SLOTS[1:]):
            m.start(('kv', o), packed.at[s + 1], mine.at[here], pos.dev(*o))

    def send_down(k):
        line, w = downs[k]
        for t in AWAY:
            m.start(('wd', k, t), cols_of(wd, line, t), w.at[slot_back(t), pos.c], line.dev(t))

    def forward_down(k):
        line, w = downs[k]
        for t in AWAY:
            m.recv(('wd', k, t))
            forward(('wd', k, t), w.at[slot_back(t), pos.c])

    send_down(0)
    send_kv()
    for k in HALVES:
        for t in STEPS:
            m.recv(('to partner', ('wo', k, t)))

    def project(ctx, w, total, first, last):
        @pl.loop(0, len(tiles(colb)))
        def _(i):
            cols = tile_of(i)
            acc = sum(jnp.dot(ctx[j], w[j, :, cols], preferred_element_type=f32) for j in range(first, last))
            total[:, cols] = total[:, cols] + acc if first else acc

    n_rows = sum_x.shape[0] // 4
    for line, ctx, w, total, *_ in lines:
        project(ctx, w, total, 0, 3)
    for line, ctx, w, total, other, got in lines:
        line.share_last('ctx')
        project(ctx, w, total, 3, 4)
        other.scatter_begin(total, got, n_rows)
    send_down(1)
    for line, ctx, w, total, other, got in lines:
        other.scatter_middle(total, got, n_rows)
    forward_gate_up(n_slots)
    forward_down(0)
    for k, (line, ctx, w, total, other, got) in enumerate(lines):
        other.scatter_last(total, got, n_rows)
        for t in AWAY:
            m.recv(('x', k, t))
        for i, t in enumerate(STEPS):
            lo = pl.multiple_of(line.index(t) * half, half)
            x_mid[k, pl.ds(lo, half), :] = (x_parts[k, i].astype(f32) + total[other.block(0, n_rows, lo, half), :]).astype(bf16)
    forward_down(1)
    local.wait('kv')

    m.finish()


def mlp_kernel(piece, gain_rows, wgu_hbm, wdx_hbm, wdy_hbm, out,
               mid_x, mid_y, normed, wgu, wd_x, wd_y, act_x, act_y, sum_x, sum_y, got_x, got_y, fin, sems, l_sem):
    pos = Place(4)
    f32, bf16 = jnp.float32, jnp.bfloat16
    width = out.shape[1]
    n_rows, colb = piece.shape[1:]
    half_rows = n_rows // 4
    ffb = act_x.shape[2]
    m, local = Msgs(sems), Local(l_sem)
    line_x, line_y = Line(pos, m, 'x'), Line(pos, m, 'y')
    sets = ((mid_x, line_y, line_x, act_x, wd_x, sum_x, got_x), (mid_y, line_x, line_y, act_y, wd_y, sum_y, got_y))

    def blk(p, lo, n):
        y, x = lax.div(p, pos.side), lax.rem(p, pos.side)
        r, c, ref, lo = (y, x, mid_x, lo) if lo < colb else (x, y, mid_y, lo - colb)
        return ref.at[pl.ds(pl.multiple_of(r * n_rows, n_rows), n_rows), pl.ds(pl.multiple_of(c * colb + lo, LANES), n)]

    here = pos.chip(0, 0)
    for k in HALVES:
        local.start(('piece', k), piece.at[k], blk(here, k * colb, colb))
    local.start('wgu', wgu_hbm, wgu)
    local.start(('wd', 0), wdx_hbm, wd_x)
    local.start(('wd', 1), wdy_hbm, wd_y)
    barrier([line.dev(t) for line in (line_x, line_y) for t in AWAY])
    local.wait(('piece', 0), ('piece', 1))
    gather = Gather(pos, m, blk, 2 * colb, by_chip=True)

    def gate_up(v, some=HALVES):
        for k in some:
            mid, sline, *_ = sets[k]

            @pl.loop(0, n_rows // CHUNK, unroll=2)
            def _(j):
                x = mid[sline.block(v, n_rows, j * CHUNK, CHUNK), :].astype(f32)
                normed[chunk(j, k * n_rows), :] = norm_rows(x, gain_rows[1:2, :])

        @pl.loop(0, len(tiles(ffb)))
        def _(i):
            mine = pl.ds(some[0] * n_rows, len(some) * n_rows)
            g, u = (jnp.dot(normed[mine, :], wgu[:, :, :, tile_of(i, base)].reshape(width, -1), preferred_element_type=f32)
                    for base in (0, ffb))
            a = (jax.nn.silu(g) * u).astype(bf16)
            for i_k, k in enumerate(some):
                mid, sline, gline, act, *_ = sets[k]
                act[0, sline.block(v, n_rows), tile_of(i)] = a[i_k * n_rows:(i_k + 1) * n_rows]

    def share(v, some=HALVES):
        for mid, sline, gline, act, *_ in (sets[k] for k in some):
            rows = sline.block(v, n_rows)
            gline.share(act, v, rows)
            if v == 2:
                gline.start(('direct', v), act.at[0, rows], act.at[slot_back(2), rows], 2)

    def share_on(v):
        for mid, sline, gline, act, *_ in sets:
            gline.share_on(act, v, lambda cut: sline.block(v, n_rows, *cut(n_rows)))

    def down(v):
        at = STEPS.index(v)
        for mid, sline, gline, act, w, total, got in sets:
            if v == 2:
                for sign in SIGNS:
                    gline.recv('share', sign, v)
                gline.recv('direct', v)
            else:
                gline.share_last(v)

            @pl.loop(0, len(tiles(colb)))
            def _(i):
                total[at, :, tile_of(i)] = sum(
                    jnp.dot(act[t, sline.block(v, n_rows), :], w[t, :, :, tile_of(i)].reshape(ffb, -1), preferred_element_type=f32)
                    for t in range(len(STEPS)))

            if v != 0:
                sline.start(('sum', v), total.at[at], got.at[slot_back(v) - 1], v)

    gather.begin()
    local.wait('wgu')
    gate_up(0)
    share(0)
    gather.forward()
    gate_up(1)
    share(1)
    share_on(0)
    gate_up(-1)
    share(-1)
    share_on(1)
    for a in STEPS:
        gather.last(a)
    share_on(-1)
    for k in HALVES:
        gate_up(2, (k,))
        share(2, (k,))
    local.wait(('wd', 0), ('wd', 1))
    for v in (1, -1, 2, 0):
        down(v)
    for k, (mid, sline, gline, act, w, total, got) in enumerate(sets):
        for v in AWAY:
            sline.recv('sum', v)
        cols = gline.lanes(0, colb)

        @pl.loop(0, n_rows // CHUNK)
        def _(j):
            rows = chunk(j)
            x = mid[sline.block(0, n_rows, j * CHUNK, CHUNK), cols].astype(f32)
            fin[k, rows, :] = (x + (total[0, rows, :] + sum(got[i, rows, :] for i in range(len(AWAY))))).astype(bf16)

        mine_rows = pl.ds(k * half_rows, half_rows)
        for t in AWAY:
            gline.start(('out', t), fin.at[k, gline.block(t, half_rows)], out.at[mine_rows, cols], t)
        out[mine_rows, cols] = fin[k, gline.block(0, half_rows), :]
    m.finish()


def dma(n):
    return pltpu.SemaphoreType.DMA((n,))


def dma2(n):
    return pltpu.SemaphoreType.DMA((2, n))


def params(cid):
    return pltpu.CompilerParams(collective_id=cid, has_side_effects=True, vmem_limit_bytes=VMEM_LIMIT)


def rope_tables(rope_scale, seq_len, lanes):
    half_dim = rope_scale.shape[0]
    freq_expo = jnp.arange(half_dim, dtype=jnp.float32) * (2.0 / (2 * half_dim))
    inv_freq = 1.0 / (rope_scale * jnp.power(ROPE_THETA, freq_expo))
    angles = jnp.arange(seq_len, dtype=jnp.float32)[:, None] * inv_freq[None, :]
    cos, sin = jnp.cos(angles), jnp.sin(angles)
    rest = jnp.zeros((seq_len, lanes - 2 * half_dim), jnp.float32)
    return jnp.concatenate([cos, cos, rest], axis=1), jnp.concatenate([-sin, sin, rest], axis=1)


def solution(mesh):
    batch_axes = ('dp', AXIS)
    row_spec = P(AXIS, None)
    n_dev = mesh.shape[AXIS]
    chips = n_dev // 2
    n_off = chips - 1

    def device_step(tokens, embed_table, norm_attn, w_qkv, w_out, norm_mlp, w_gate_up, w_down, rope_scale):
        f32, bf16 = jnp.float32, jnp.bfloat16
        seq = tokens.shape[1]
        rows, d_model = w_out.shape
        head_dim = 2 * rope_scale.shape[0]
        ffb = w_gate_up.shape[1] // (2 * chips)
        qkv_width = w_qkv.shape[1] // chips
        wide = pl.cdiv(qkv_width + 2, LANES) * LANES
        toks, half_toks, colb = chips * seq, chips * seq // 2, d_model // 4
        tok = jnp.zeros((8, LANES), jnp.int32) + jnp.pad(tokens, ((0, 0), (0, LANES - seq)))
        column = lax.broadcasted_iota(jnp.int32, (rows, wide - qkv_width), 1)
        gains = (jnp.where(column == 0, norm_attn[:, None], 0) + jnp.where(column == 1, norm_mlp[:, None], 0)).astype(bf16)
        cos2, sin2 = rope_tables(rope_scale, seq, LANES)
        vmem = pl.BlockSpec(memory_space=pltpu.VMEM)
        shape = jax.ShapeDtypeStruct

        def buf(*dims, dtype=bf16):
            return pltpu.VMEM(dims, dtype)

        wgu_shape = (chips, 2, rows, 2 * ffb)
        wd_shape = (4, 2, ffb // 2, colb)
        kv_shape = (chips, seq, 4 * head_dim)
        sum_blocks = half_toks // 4
        x_mid, mine, wgu_all, wd_x, wd_y, gain_rows = pl.pallas_call(
            front_kernel, name='front',
            out_shape=(shape((2, sum_blocks, colb), bf16), shape(kv_shape, bf16), shape(wgu_shape, bf16),
                       shape(wd_shape, bf16), shape(wd_shape, bf16), shape((8, d_model), f32)),
            in_specs=[ANY] + [vmem] * 4 + [ANY] * 4, out_specs=(vmem, ANY, ANY, ANY, ANY, vmem),
            scratch_shapes=[buf(*kv_shape), buf(chips, 8, LANES, dtype=jnp.int32), buf(toks, 1, dtype=f32), buf(2, *embed_table.shape),
                            buf(2, toks // 4, embed_table.shape[0]), buf(toks, d_model), buf(seq, d_model * n_off),
                            buf(toks, d_model), buf(chips, rows, wide), buf(d_model, wide), buf(2, 4, seq // 2, colb),
                            buf(5 * seq, wide, dtype=f32)]
                           + [buf(4, half_toks, 2 * LANES)] * 2 + [buf(4, 2 * LANES, colb)] * 2
                           + [buf(half_toks, colb, dtype=f32)] * 2 + [buf(3 * sum_blocks, colb, dtype=f32)] * 2
                           + [dma2(240), dma(9)],
            compiler_params=params(1),
        )(tok, gains, w_qkv, cos2, sin2, w_gate_up, w_out, w_down, embed_table)

        layer_out = pl.pallas_call(
            mlp_kernel, name='mlp',
            out_shape=shape((seq, d_model), bf16),
            in_specs=[ANY, vmem] + [ANY] * 3, out_specs=vmem,
            scratch_shapes=[buf(half_toks, d_model)] * 2 + [buf(half_toks // 2, d_model), buf(*wgu_shape)]
                           + [buf(*wd_shape)] * 2 + [buf(4, half_toks, ffb)] * 2
                           + [buf(4, sum_blocks, colb, dtype=f32)] * 2 + [buf(3, sum_blocks, colb, dtype=f32)] * 2
                           + [buf(2, sum_blocks, colb), dma2(84), dma(5)],
            compiler_params=params(2),
        )(x_mid, gain_rows, wgu_all, wd_x, wd_y)

        def by_head(lo):
            part = mine[:, :, lo:lo + 2 * head_dim].transpose(1, 0, 2)
            return part.reshape(1, seq, 2 * chips, head_dim)

        key_own, val_own = by_head(0), by_head(2 * head_dim)
        return layer_out[None], key_own, val_own

    return jax.shard_map(
        device_step,
        mesh=mesh,
        in_specs=(P(batch_axes, None), row_spec, P(AXIS), row_spec, row_spec, P(AXIS), row_spec, row_spec, P(None)),
        out_specs=(P(batch_axes, None, None), P(batch_axes, None, None, None), P(batch_axes, None, None, None)),
        check_vma=False,
    )
```

time: 887 us -> 297 us (0.33)
  waiting for transfers between devices: 651 us -> 0 us
  Pallas kernels: 0 us -> 288 us
  matrix products: 88.9 us -> 0 us
  blocking collectives: 79 us -> 0 us
  local copies, waits for them, and re-layouts: 35.7 us -> 5.13 us
  between operations: 14 us -> 0.69 us
  other arithmetic: 15.3 us -> 2.9 us
    all_gather x4 -> x0, waiting for transfers between devices: 600 us -> none  [gather_rows(): return lax.all_gather(weight, 'fsdp', axis=0, tiled=True)]
    pallas_call x0 -> x2, Pallas kernels: none -> 288 us  [the longest x1 204 us: device_step(): pl.pallas_call(front_kernel, name='front', out_shape=(shape((2, sum_block...]
    dot_general x6 -> x0, matrix products: 88.9 us -> none  [the longest x1 36.7 us: decoder_layer(): jnp.einsum('bld,df->blf', normed_mlp, w_gate_up, preferred_element_type=j...]
    reduce_scatter x1 -> x0, waiting for transfers between devices: 48.9 us -> none  [device_step(): lax.psum_scatter(table_rows, 'fsdp', scatter_dimension=0, tiled=True)]
    unnamed x1 -> x0, blocking collectives: 42.8 us -> none
    all_gather x1 -> x0, blocking collectives: 36.2 us -> none  [device_step(): group_tokens = lax.all_gather(tokens, 'fsdp', axis=0, tiled=True)]
    gather x1 -> x0, local copies, waits for them, and re-layouts: 26.5 us -> none  [device_step(): jnp.take(embed_table, jnp.clip(local_ids, 0, shard_rows - 1), axis=0)]
    select_n x1 -> x0, other arithmetic: 10.9 us -> none  [device_step(): jnp.where(owned_mask[..., None], table_rows, jnp.zeros((), table_rows.dty...]
  transfers between devices with their start and end apart: 5 -> 0, of which waited for: 5 -> 0; matrix products, arithmetic and copies ran while one was open for 9% -> 0% of each run, Pallas kernels for 0% -> 0%
where the time goes in v5:
time: 297 us
  Pallas kernels  288 us (97%)
  local copies, waits for them, and re-layouts  5.13 us (2%)
    pallas_call x1, Pallas kernels, device_step(): pl.pallas_call(front_kernel, name='front', out_shape=(shape((2, sum_block...  204 us
    pallas_call x1, Pallas kernels, device_step(): pl.pallas_call(mlp_kernel, name='mlp', out_shape=shape((seq, d_model), bf...  83.6 us

profile of v5, /device:TPU:96, one launch (start us, length us, event | category | flops | bytes accessed | tf_op | source)
XLA Modules:
  0.0 296.6 jit_solution(2355517339014548058)
XLA Ops:
  0.6 0.7 pad_bitcast_fusion
  1.3 0.7 multiply_divide_fusion
  2.0 0.1 pad.10.clone
  2.0 0.6 add.13.tok
  2.6 1.4 select_add_fusion.gains
  4.0 0.1 fusion.2
  4.2 0.7 maximum_maximum_fusion.1
  4.9 204.2 %front.1 = (bf16[2,128,768]{2,1,0:T(8,128)(2,1)}, bf16[16,64,384]{2,1,0:T(8,128)(2,1)}, bf16[16,2,96,1024]{3,2,1,0:T(8,128)(2,1)}, bf16[4,2,256,768]{3,2,1,0:T(8...) custom-call(s32[8,128]{1,0:T(8,128)} %add.13.tok, bf16[96,64]{1,0:T(8,128)(2,1)} %select_add_fusion.gains, ...), custom_call_target="tpu_custom_call" | custom-call | tf_op jit(solution)/shard_map/front/pallas_call | solution.py:718
  209.1 0.0 copy-start.1
  209.1 83.6 %mlp.1 = bf16[64,3072]{1,0:T(8,128)(2,1)} custom-call(bf16[2,128,768]{2,1,0:T(8,128)(2,1)} %get-tuple-element.9.piece, f32[8,3072]{1,0:T(8,128)} %get-tuple-element.10.gain_rows, bf16[16,2,96,1024]{3,2,1,0:T(8,128)(2,1)} %get-tuple-element.11.wgu_hbm, bf16[4,2,256,768]{3,2,1,0:T(8,128)(2,1)} %get-tuple-element.12.wdx_hbm, ...), custom_call_target="tpu_custom_call" | custom-call | tf_op jit(solution)/shard_map/mlp/pallas_call | solution.py:733
  292.7 0.0 copy-done.1
  292.7 0.0 copy-start
  292.8 0.3 slice_bitcast_fusion
  293.0 0.3 copy.13
  293.3 1.1 reshape.16
  294.4 0.3 copy.12
  294.7 1.1 reshape.15
  295.8 0.0 copy-done
  295.8 0.7 copy.15
  (2 shorter events, 0.0 us)
Async XLA Ops:
  209.1 83.6 %copy-start.1 = (bf16[16,64,384]{2,1,0:T(8,128)(2,1)S(1)}, bf16[16,64,384]{2,1,0:T(8,128)(2,1)}, u32[]{:S(2)}) copy-start(bf16[16,64,384]{2,1,0:T(8,128)(2,1)} %get-tuple-element.14) | copy-start | bytes 2359300
  292.7 3.1 %copy-start = (bf16[64,3072]{1,0:T(8,128)(2,1)S(1)}, bf16[64,3072]{1,0:T(8,128)(2,1)}, u32[]{:S(2)}) copy-start(bf16[64,3072]{1,0:T(8,128)(2,1)} %mlp.1) | copy-start | bytes 1179652

commit v6 on v5

--- a/solution.py
+++ b/solution.py
@@ -298,9 +298,9 @@
     return pl.ds(pl.multiple_of(base + i * tile, LANES), tile)
 
 
-def front_kernel(tok, gains, wqkv, cos2, sin2, wgu, wo, wd, table,
+def front_kernel(tok, gain_attn, gain_mlp, wqkv, cos2, sin2, wgu, wo, wd, table,
                  x_mid, mine, wgu_all, wd_x, wd_y, gain_rows,
-                 packed, tok_all, tok_col, tbl, hot, part, recv_buf, h_all, wq_out, wq, x_parts, proj,
+                 packed, tok_own, gain_own, tok_all, tok_col, tbl, hot, part, recv_buf, h_all, wq_out, wq, x_parts, proj,
                  ctx_x, ctx_y, wo_x, wo_y, sum_x, sum_y, got_x, got_y, sems, l_sem):
     f32, bf16 = jnp.float32, jnp.bfloat16
     pos = Place(4)
@@ -330,17 +330,19 @@
         return wgu_all.at[here, pos.c, :, pl.ds(j * ffb, ffb)]
 
     local.start('table', table, tbl.at[pos.c])
-    local.start('tok', tok, tok_all.at[0])
     for k, (line, ctx, w, *_) in enumerate(lines):
         local.start(('wo', k), cols_of(wo, line, 0), w.at[0, my_head])
     for k, (line, w) in enumerate(downs):
         local.start(('wd', k), cols_of(wd, line, 0), w.at[0, pos.c])
     for j in HALVES:
         local.start(('wgu', j), gate_up_block(j, here), gate_up_place(j))
+    tok_own[...] = jnp.zeros_like(tok_own)
+    tok_own[0:1, 0:seq] = tok[...]
+    tok_all[0] = tok_own[...]
     barrier([pos.dev(*o) for o in offs] + [pos.partner])
 
     for o in offs:
-        m.start(('tok', o), tok, tok_all.at[slot_of(-o[0], -o[1])], pos.dev(*o))
+        m.start(('tok', o), tok_own, tok_all.at[slot_of(-o[0], -o[1])], pos.dev(*o))
     m.start('table', table, tbl.at[pos.c], pos.partner)
     to_send = list(offs)
 
@@ -350,15 +352,20 @@
             for j in HALVES:
                 m.start(('wgu', j, o), gate_up_block(j, pos.chip(*o)), gate_up_place(j), pos.dev(*o))
 
-    send_gate_up(3)
+    send_gate_up(6)
     blank = jnp.zeros((len(STEPS), LANES - rows, colb), bf16)
     for w in (wo_x, wo_y):
         for hd in HALVES:
             w[:, hd * LANES + rows:(hd + 1) * LANES, :] = blank
     block = 2 * head_dim
+    gain_own[...] = jnp.zeros_like(gain_own)
+    for i, gain in enumerate((gain_attn, gain_mlp)):
+        gain_own[i:i + 1, 0:rows] = gain[...].astype(f32)
+    gains = jnp.transpose(gain_own[...])[:rows].astype(bf16)
+    gains = jnp.concatenate([gains, jnp.zeros((rows, wq.shape[1] - 3 * block - gains.shape[1]), bf16)], axis=1)
     for p in range(n_slots):
         pieces = [wqkv[:, (j * n_slots + p) * block:(j * n_slots + p + 1) * block] for j in range(3)]
-        wq_out[p] = jnp.concatenate(pieces + [gains[...]], axis=1)
+        wq_out[p] = jnp.concatenate(pieces + [gains], axis=1)
     for o in offs:
         m.start(('wq', o), wq_out.at[pos.chip(*o)], wq.at[my_rows], pos.dev(*o))
     for k, (line, ctx, w, *_) in enumerate(lines):
@@ -366,7 +373,6 @@
             m.start(('wo', k, t), cols_of(wo, line, t), w.at[slot_back(t), my_head], line.dev(t))
     wq[my_rows, :] = wq_out[here]
 
-    local.wait('tok')
     for o in offs:
         m.recv(('tok', o))
     for s in range(n_slots):
@@ -701,9 +707,6 @@
         qkv_width = w_qkv.shape[1] // chips
         wide = pl.cdiv(qkv_width + 2, LANES) * LANES
         toks, half_toks, colb = chips * seq, chips * seq // 2, d_model // 4
-        tok = jnp.zeros((8, LANES), jnp.int32) + jnp.pad(tokens, ((0, 0), (0, LANES - seq)))
-        column = lax.broadcasted_iota(jnp.int32, (rows, wide - qkv_width), 1)
-        gains = (jnp.where(column == 0, norm_attn[:, None], 0) + jnp.where(column == 1, norm_mlp[:, None], 0)).astype(bf16)
         cos2, sin2 = rope_tables(rope_scale, seq, LANES)
         vmem = pl.BlockSpec(memory_space=pltpu.VMEM)
         shape = jax.ShapeDtypeStruct
@@ -719,16 +722,16 @@
             front_kernel, name='front',
             out_shape=(shape((2, sum_blocks, colb), bf16), shape(kv_shape, bf16), shape(wgu_shape, bf16),
                        shape(wd_shape, bf16), shape(wd_shape, bf16), shape((8, d_model), f32)),
-            in_specs=[ANY] + [vmem] * 4 + [ANY] * 4, out_specs=(vmem, ANY, ANY, ANY, ANY, vmem),
-            scratch_shapes=[buf(*kv_shape), buf(chips, 8, LANES, dtype=jnp.int32), buf(toks, 1, dtype=f32), buf(2, *embed_table.shape),
+            in_specs=[vmem] * 6 + [ANY] * 4, out_specs=(vmem, ANY, ANY, ANY, ANY, vmem),
+            scratch_shapes=[buf(*kv_shape), buf(8, LANES, dtype=jnp.int32), buf(8, LANES, dtype=f32), buf(chips, 8, LANES, dtype=jnp.int32), buf(toks, 1, dtype=f32), buf(2, *embed_table.shape),
                             buf(2, toks // 4, embed_table.shape[0]), buf(toks, d_model), buf(seq, d_model * n_off),
                             buf(toks, d_model), buf(chips, rows, wide), buf(d_model, wide), buf(2, 4, seq // 2, colb),
                             buf(5 * seq, wide, dtype=f32)]
                            + [buf(4, half_toks, 2 * LANES)] * 2 + [buf(4, 2 * LANES, colb)] * 2
                            + [buf(half_toks, colb, dtype=f32)] * 2 + [buf(3 * sum_blocks, colb, dtype=f32)] * 2
-                           + [dma2(240), dma(9)],
+                           + [dma2(240), dma(8)],
             compiler_params=params(1),
-        )(tok, gains, w_qkv, cos2, sin2, w_gate_up, w_out, w_down, embed_table)
+        )(tokens, norm_attn[None], norm_mlp[None], w_qkv, cos2, sin2, w_gate_up, w_out, w_down, embed_table)
 
         layer_out = pl.pallas_call(
             mlp_kernel, name='mlp',

time: 297 us -> 292 us (0.983)
  no operation moved by 1% of the time
where the time goes in v6:
time: 292 us
  Pallas kernels  286 us (98%)
  local copies, waits for them, and re-layouts  3.87 us (1%)
    pallas_call x1, Pallas kernels, device_step(): pl.pallas_call(front_kernel, name='front', out_shape=(shape((2, sum_block...  202 us
    pallas_call x1, Pallas kernels, device_step(): pl.pallas_call(mlp_kernel, name='mlp', out_shape=shape((seq, d_model), bf...  83.5 us

profile of v6, /device:TPU:96, one launch (start us, length us, event | category | flops | bytes accessed | tf_op | source)
XLA Modules:
  0.0 292.1 jit_solution(5590803436634696219)
XLA Ops:
  0.6 0.7 multiply_divide_fusion
  1.3 0.1 pad.5.clone
  1.4 0.1 fusion.2
  1.5 0.7 maximum_maximum_fusion.1
  2.2 202.5 %front.1 = (bf16[2,128,768]{2,1,0:T(8,128)(2,1)}, bf16[16,64,384]{2,1,0:T(8,128)(2,1)}, bf16[16,2,96,1024]{3,2,1,0:T(8,128)(2,1)}, bf16[4,2,256,768]{3,2,1,0:T(8...) custom-call(s32[1,64]{1,0:T(1,128)} %tok.1, bf16[1,96]{1,0:T(2,128)(2,1)} %bitcast.8, ...), custom_call_target="tpu_custom_call" | custom-call | tf_op jit(solution)/shard_map/front/pallas_call | solution.py:721
  204.7 0.0 copy-start.1
  204.7 83.5 %mlp.1 = bf16[64,3072]{1,0:T(8,128)(2,1)} custom-call(bf16[2,128,768]{2,1,0:T(8,128)(2,1)} %get-tuple-element.9.piece, f32[8,3072]{1,0:T(8,128)} %get-tuple-element.10.gain_rows, bf16[16,2,96,1024]{3,2,1,0:T(8,128)(2,1)} %get-tuple-element.11.wgu_hbm, bf16[4,2,256,768]{3,2,1,0:T(8,128)(2,1)} %get-tuple-element.12.wdx_hbm, ...), custom_call_target="tpu_custom_call" | custom-call | tf_op jit(solution)/shard_map/mlp/pallas_call | solution.py:736
  288.3 0.0 copy-done.1
  288.3 0.0 copy-start
  288.3 0.3 slice_bitcast_fusion
  288.6 0.3 copy.13
  288.9 1.1 reshape.14
  290.0 0.3 copy.12
  290.3 1.1 reshape.13
  291.4 0.0 copy-done
  291.4 0.7 copy.15
  (1 shorter events, 0.0 us)
Async XLA Ops:
  204.7 83.6 %copy-start.1 = (bf16[16,64,384]{2,1,0:T(8,128)(2,1)S(1)}, bf16[16,64,384]{2,1,0:T(8,128)(2,1)}, u32[]{:S(2)}) copy-start(bf16[16,64,384]{2,1,0:T(8,128)(2,1)} %get-tuple-element.14) | copy-start | bytes 2359300
  288.3 3.1 %copy-start = (bf16[64,3072]{1,0:T(8,128)(2,1)S(1)}, bf16[64,3072]{1,0:T(8,128)(2,1)}, u32[]{:S(2)}) copy-start(bf16[64,3072]{1,0:T(8,128)(2,1)} %mlp.1) | copy-start | bytes 1179652

commit v7 on v6

--- a/solution.py
+++ b/solution.py
@@ -410,7 +410,7 @@
         square = jnp.transpose(wq[pl.ds(lo, n), qkv_width // LANES * LANES:].astype(f32))
         gain_rows[:, lo:lo + n] = square[qkv_width % LANES:qkv_width % LANES + gain_rows.shape[0], :]
 
-    scatter.finish(lambda i: send_gate_up(1 if 5 < i < 14 else 0))
+    scatter.finish(lambda i: send_gate_up(1 if 6 < i else 0))
 
     @pl.loop(0, seq // CHUNK)
     def _(i):
@@ -475,6 +475,22 @@
                 m.recv(('wgu', j, o))
             forward(('wgu', o), wgu_all.at[pos.chip(-o[0], -o[1]), pos.c])
 
+    def send_kv():
+        local.start('kv', packed.at[0], mine.at[here])
+        for s, o in enumerate(SLOTS[1:]):
+            m.start(('kv', o), packed.at[s + 1], mine.at[here], pos.dev(*o))
+
+    def send_down(*offsets_sent):
+        for t in offsets_sent:
+            for k, (line, w) in enumerate(downs):
+                m.start(('wd', k, t), cols_of(wd, line, t), w.at[slot_back(t), pos.c], line.dev(t))
+
+    def forward_down(k):
+        line, w = downs[k]
+        for t in AWAY:
+            m.recv(('wd', k, t))
+            forward(('wd', k, t), w.at[slot_back(t), pos.c])
+
     gather.begin()
     attend(0, 5)
     for a in (-1, 1):
@@ -489,11 +505,9 @@
     send_gate_up(n_slots)
     gather.last(0)
     attend(9, 2)
-    for a in (-1, 1):
+    for a in AWAY:
         gather.last(a)
-    attend(11, 4)
-    gather.last(2)
-    attend(15, 1)
+    attend(11, 5)
 
     every = pl.ds(*whole(ctx_x.shape[1]))
     for line, ctx, *_ in lines:
@@ -501,24 +515,7 @@
     for line, ctx, *_ in lines:
         line.share_on(ctx, 'ctx', lambda cut: pl.ds(*cut(ctx_x.shape[1])))
 
-    def send_kv():
-        local.start('kv', packed.at[0], mine.at[here])
-        for s, o in enumerate(SLOTS[1:]):
-            m.start(('kv', o), packed.at[s + 1], mine.at[here], pos.dev(*o))
-
-    def send_down(k):
-        line, w = downs[k]
-        for t in AWAY:
-            m.start(('wd', k, t), cols_of(wd, line, t), w.at[slot_back(t), pos.c], line.dev(t))
-
-    def forward_down(k):
-        line, w = downs[k]
-        for t in AWAY:
-            m.recv(('wd', k, t))
-            forward(('wd', k, t), w.at[slot_back(t), pos.c])
-
-    send_down(0)
-    send_kv()
+    send_down(1, -1)
     for k in HALVES:
         for t in STEPS:
             m.recv(('to partner', ('wo', k, t)))
@@ -537,7 +534,8 @@
         line.share_last('ctx')
         project(ctx, w, total, 3, 4)
         other.scatter_begin(total, got, n_rows)
-    send_down(1)
+    send_down(2)
+    send_kv()
     for line, ctx, w, total, other, got in lines:
         other.scatter_middle(total, got, n_rows)
     forward_gate_up(n_slots)

time: 292 us -> 293 us (level)
  no operation moved by 1% of the time
where the time goes in v7:
time: 293 us
  Pallas kernels  287 us (98%)
  local copies, waits for them, and re-layouts  3.87 us (1%)
    pallas_call x1, Pallas kernels, device_step(): pl.pallas_call(front_kernel, name='front', out_shape=(shape((2, sum_block...  204 us
    pallas_call x1, Pallas kernels, device_step(): pl.pallas_call(mlp_kernel, name='mlp', out_shape=shape((seq, d_model), bf...  83.2 us

profile of v7, /device:TPU:96, one launch (start us, length us, event | category | flops | bytes accessed | tf_op | source)
XLA Modules:
  0.0 293.2 jit_solution(1635716525396247647)
XLA Ops:
  0.6 0.7 multiply_divide_fusion
  1.3 0.1 pad.5.clone
  1.4 0.1 fusion.2
  1.5 0.7 maximum_maximum_fusion.1
  2.2 204.0 %front.1 = (bf16[2,128,768]{2,1,0:T(8,128)(2,1)}, bf16[16,64,384]{2,1,0:T(8,128)(2,1)}, bf16[16,2,96,1024]{3,2,1,0:T(8,128)(2,1)}, bf16[4,2,256,768]{3,2,1,0:T(8...) custom-call(s32[1,64]{1,0:T(1,128)} %tok.1, bf16[1,96]{1,0:T(2,128)(2,1)} %bitcast.8, ...), custom_call_target="tpu_custom_call" | custom-call | tf_op jit(solution)/shard_map/front/pallas_call | solution.py:719
  206.2 0.0 copy-start.1
  206.2 83.2 %mlp.1 = bf16[64,3072]{1,0:T(8,128)(2,1)} custom-call(bf16[2,128,768]{2,1,0:T(8,128)(2,1)} %get-tuple-element.9.piece, f32[8,3072]{1,0:T(8,128)} %get-tuple-element.10.gain_rows, bf16[16,2,96,1024]{3,2,1,0:T(8,128)(2,1)} %get-tuple-element.11.wgu_hbm, bf16[4,2,256,768]{3,2,1,0:T(8,128)(2,1)} %get-tuple-element.12.wdx_hbm, ...), custom_call_target="tpu_custom_call" | custom-call | tf_op jit(solution)/shard_map/mlp/pallas_call | solution.py:734
  289.4 0.0 copy-done.1
  289.4 0.0 copy-start
  289.4 0.3 slice_bitcast_fusion
  289.7 0.3 copy.13
  290.0 1.1 reshape.14
  291.1 0.3 copy.12
  291.4 1.1 reshape.13
  292.5 0.0 copy-done
  292.5 0.7 copy.15
  (1 shorter events, 0.0 us)
Async XLA Ops:
  206.2 83.2 %copy-start.1 = (bf16[16,64,384]{2,1,0:T(8,128)(2,1)S(1)}, bf16[16,64,384]{2,1,0:T(8,128)(2,1)}, u32[]{:S(2)}) copy-start(bf16[16,64,384]{2,1,0:T(8,128)(2,1)} %get-tuple-element.14) | copy-start | bytes 2359300
  289.4 3.1 %copy-start = (bf16[64,3072]{1,0:T(8,128)(2,1)S(1)}, bf16[64,3072]{1,0:T(8,128)(2,1)}, u32[]{:S(2)}) copy-start(bf16[64,3072]{1,0:T(8,128)(2,1)} %mlp.1) | copy-start | bytes 1179652
